TPU v7x, 32 devices: a whole 2x2x4 slice. The times are simulated.
32 devices in a mesh: heads: 4 (over y, core), blk: 8 (over z, x).
Axes of the slice: x: 2, y: 2, z: 4, core: 2. Of those that a mesh axis runs over, the one named last changes fastest.
Arguments:
- tokens: bfloat16 [4096, 4096], P(('blk', 'heads')), may hold values from -6 to 6
- w_query: bfloat16 [4096, 2048], P('blk', 'heads'), may hold values from -0.75 to 0.75
- key_value_weight: bfloat16 [4096, 2, 512], P('blk', None, 'heads'), may hold values from -0.75 to 0.75
- w_out: bfloat16 [2048, 4096], P(('heads', 'blk')), may hold values from -0.5 to 0.5
- doc_lengths: int32 [16], replicated, may hold values from 1 to 1024, 4096 in all
Outputs:
- attended: bfloat16 [4096, 4096], P(('blk', 'heads'))
Inputs may be any that keep to these rules, and one draw needn't show every extreme that they name: `doc_lengths`: the 16 lengths sum to 4096; the longest document has exactly 1024 tokens.
All inputs are finite; a program needn't handle non-finite values.
Results may differ from a plain program's by a relative error of at most 0.012.
Values may be sent and summed in bfloat16 or wider, within the bound.
A program may use at most 128 MiB of HBM per device.

v0:
```python
import functools

import jax
import jax.numpy as jnp
import numpy as np
from jax import lax
from jax.experimental import pallas as pl
from jax.experimental.pallas import tpu as pltpu
from jax.sharding import PartitionSpec as P

HEAD_SIZE = 128
CHUNKS = 4
LINE = 2

norm_epsilon = 1e-05
rope_base = 500000.0
masked_score = -1e30
MESH = pl.DeviceIdType.MESH
UP, DOWN, ACROSS = 0, 1, 2
QUERY, KEYVAL = -1, -2


def layer_kernel(
    n, heads, chunks,
    tok_ref, w_query_ref, w_keyval_ref, w_out_ref, len_ref, freq_ref, out_ref,
    w_in, w_kv, w_proj, acts, qkv, query, kv, high, total, accum, mixed, rope,
    near_send, near_recv, part, far_send, far_recv,
    local_sem, in_send, in_recv, proj_send, proj_recv, bal_send,
    act_send, act_recv, kv_send, kv_recv, near_ss, near_rs, far_ss, far_rs,
):
    f32, bf16 = jnp.float32, jnp.bfloat16
    b = lax.axis_index("blk")
    h = lax.axis_index("heads")
    steps = n // LINE
    z, x = b // LINE, b % LINE
    outer = heads // 2
    y, core = h // 2, h % 2
    mate = y * 2 + 1 - core
    reach = n // 4
    tokens_own, width = tok_ref.shape
    rows_in = w_query_ref.shape[0]
    rows_out = w_out_ref.shape[0]
    chunk_cols = w_out_ref.shape[1] // chunks
    block = tokens_own * heads
    q_cols = query.shape[1]
    q_heads = q_cols // HEAD_SIZE

    def at_blk(i):
        return {"blk": i}

    def at_head(i):
        return {"heads": i}

    def remote(src, dst, ss, rs, dev):
        return pltpu.make_async_remote_copy(
            src_ref=src, dst_ref=dst, send_sem=ss, recv_sem=rs, device_id=dev, device_id_type=MESH
        )

    barrier = pltpu.get_barrier_semaphore()
    span = max(reach, LINE)
    peers = 0
    for d in sorted({e % n for k in range(1, span + 1) for e in (k, -k)}):
        pl.semaphore_signal(barrier, inc=1, device_id=at_blk(lax.rem(b + d, n)), device_id_type=MESH)
        peers += 1
    for d in range(1, heads):
        pl.semaphore_signal(barrier, inc=1, device_id=at_head(lax.rem(h + d, heads)), device_id_type=MESH)
        peers += 1
    pl.semaphore_wait(barrier, peers)

    def in_slot(i):
        return w_in.at[pl.ds(pl.multiple_of(i * rows_in, rows_in), rows_in)]

    def kv_slot(i):
        return w_kv.at[pl.ds(pl.multiple_of(i * rows_in, rows_in), rows_in)]

    def proj_slot(c, i):
        return w_proj.at[c, i]

    def proj_own(c):
        return w_out_ref.at[:, pl.ds(c * chunk_cols, chunk_cols)]

    def stream(c):
        if c < 0:
            slot, source = (in_slot, w_query_ref) if c == QUERY else (kv_slot, kv_slot(b))
            return slot, source, lambda d, r: in_send.at[c + 2, d, r], lambda i: in_recv.at[c + 2, i]
        return (
            functools.partial(proj_slot, c), proj_own(c),
            lambda d, r: proj_send.at[c, d, r], lambda i: proj_recv.at[c, i],
        )

    def target(direction):
        if direction == UP:
            return at_blk(lax.rem(b + LINE, n))
        if direction == DOWN:
            return at_blk(lax.rem(b + n - LINE, n))
        return at_blk(z * LINE + 1 - x)

    def send_copy(c, direction, row, own):
        slot, source, ss, rs = stream(c)
        origin = row * LINE + x
        dst = slot(origin)
        return remote(source if own else dst, dst, ss(direction, row), rs(origin), target(direction))

    def await_slot(c, origin):
        slot, source, ss, rs = stream(c)
        ref = slot(origin)
        remote(ref, ref, ss(0, 0), rs(origin), target(ACROSS)).wait_recv()

    twin = z + 1 - 2 * (z % 2)

    def crosses(c, row):
        if c < 0:
            return row >= 0
        return row != twin

    def line_own(c):
        @pl.when(z < steps - 1)
        def _():
            send_copy(c, UP, z, True).start()

        @pl.when(z > 0)
        def _():
            send_copy(c, DOWN, z, True).start()

    def line_step(c, s):
        @pl.when(z - s >= 0)
        def _():
            await_slot(c, (z - s) * LINE + x)

            @pl.when(z < steps - 1)
            def _():
                send_copy(c, UP, z - s, False).start()

        @pl.when(z + s <= steps - 1)
        def _():
            await_slot(c, (z + s) * LINE + x)

            @pl.when(z > 0)
            def _():
                send_copy(c, DOWN, z + s, False).start()

    def cross_own(c):
        send_copy(c, ACROSS, z, True).start()

    def cross_step(c, s):
        @pl.when((z - s >= 0) & crosses(c, z - s))
        def _():
            send_copy(c, ACROSS, z - s, False).start()

        @pl.when((z + s <= steps - 1) & crosses(c, z + s))
        def _():
            send_copy(c, ACROSS, z + s, False).start()

    def side_copy(c):
        ref = proj_slot(c, z * LINE + 1 - x)
        return remote(ref, ref, bal_send.at[c], proj_recv.at[c, z * LINE + 1 - x],
                      at_blk(twin * LINE + x))

    def balance(c):
        @pl.when(twin < steps)
        def _():
            await_slot(c, z * LINE + 1 - x)
            side_copy(c).start()

    def await_crossed(c):
        def one(row, _):
            if c < 0:
                await_slot(c, row * LINE + 1 - x)
            else:
                @pl.when((row != z) | (twin >= steps))
                def _():
                    await_slot(c, row * LINE + 1 - x)
            return 0

        lax.fori_loop(0, steps, one, 0)

    line_own(QUERY)
    cross_own(QUERY)
    keep_in = pltpu.make_async_copy(w_query_ref, in_slot(b), local_sem.at[chunks])
    keep_in.start()
    w_kv[pl.ds(pl.multiple_of(b * rows_in, rows_in), rows_in), :] = w_keyval_ref[...].reshape(
        rows_in, w_kv.shape[1]
    )
    line_own(KEYVAL)
    cross_own(KEYVAL)
    keep_out = [
        pltpu.make_async_copy(proj_own(c), proj_slot(c, b), local_sem.at[c]) for c in range(chunks)
    ]
    for copy in keep_out:
        copy.start()

    values = tok_ref[...].astype(f32)
    acts[h] = (
        values * lax.rsqrt(jnp.mean(values * values, axis=1, keepdims=True) + norm_epsilon)
    ).astype(bf16)

    act_copies = []
    for o in range(1, outer):
        act_copies.append(remote(acts.at[h], acts.at[h], act_send.at[o], act_recv.at[h],
                                 at_head(lax.rem(y + o, outer) * 2 + core)))
    act_copies.append(remote(acts.at[h], acts.at[h], act_send.at[0], act_recv.at[h], at_head(mate)))
    for copy in act_copies:
        copy.start()

    pos = b * block + lax.broadcasted_iota(jnp.int32, (block, 1), 0)
    start = jnp.zeros((block, 1), jnp.int32)
    end = jnp.int32(0)
    for i in range(len_ref.shape[0]):
        size = len_ref[i]
        end = end + size
        start = start + jnp.where(pos >= end, size, 0)
    angle = (pos - start).astype(f32) * freq_ref[...]
    lane = lax.broadcasted_iota(jnp.int32, (block, HEAD_SIZE), 1)
    rope[0] = jnp.cos(angle)
    rope[1] = jnp.where(lane < HEAD_SIZE // 2, -jnp.sin(angle), jnp.sin(angle))

    def in_step(s, _):
        for c in (QUERY, KEYVAL):
            line_step(c, s)
            cross_step(c, s)
        return 0

    in_step(1, 0)
    for o in range(1, outer):
        other = lax.rem(y + o, outer) * 2 + core
        remote(acts.at[other], acts.at[other], act_send.at[0], act_recv.at[other], at_head(mate)).wait_recv()
        copy = remote(acts.at[other], acts.at[other], act_send.at[outer + o], act_recv.at[other], at_head(mate))
        copy.start()
        act_copies.append(copy)
    lax.fori_loop(2, steps - 1, in_step, 0)

    for c in range(chunks):
        line_own(c)
    in_step(steps - 1, 0)
    for c in range(chunks // 2):
        cross_own(c)
    line_events = [(c, s) for s in range(1, steps) for c in range(chunks)]

    def run_events(count):
        for _ in range(min(count, len(line_events))):
            c, s = line_events.pop(0)
            line_step(c, s)

    run_events(chunks + chunks // 2)

    keep_in.wait()
    await_crossed(QUERY)
    await_crossed(KEYVAL)
    for o in range(outer):
        other = lax.rem(y + o, outer) * 2 + 1 - core
        remote(acts.at[other], acts.at[other], act_send.at[0], act_recv.at[other], at_head(mate)).wait_recv()

    depth = min(512, width)

    def project(k, _):
        cols = pl.ds(pl.multiple_of(k * depth, depth), depth)
        left = acts[:, :, cols].reshape(block, depth)
        qkv[:, :q_cols] += jnp.dot(left, w_in[cols, :], preferred_element_type=f32)
        qkv[:, q_cols:] += jnp.dot(left, w_kv[cols, :], preferred_element_type=f32)
        return 0

    qkv[...] = jnp.zeros_like(qkv)
    lax.fori_loop(0, width // depth, project, 0)

    cosine, sine = rope[0], rope[1]

    def rotated(first):
        v = qkv[:, first:first + HEAD_SIZE]
        return (v * cosine + pltpu.roll(v, HEAD_SIZE // 2, 1) * sine).astype(bf16)

    kv[0, :, :HEAD_SIZE] = rotated(q_cols)
    kv[0, :, HEAD_SIZE:] = qkv[:, q_cols + HEAD_SIZE:].astype(bf16)
    for j in range(q_heads):
        query[:, j * HEAD_SIZE:(j + 1) * HEAD_SIZE] = rotated(j * HEAD_SIZE)

    def kv_copy(d):
        return remote(kv.at[0], kv.at[d], kv_send.at[d], kv_recv.at[d], at_blk(lax.rem(b + d, n)))

    def kv_start(d, _):
        @pl.when(b + d < n)
        def _():
            kv_copy(d).start()
        return 0

    lax.fori_loop(1, reach + 1, kv_start, 0)
    run_events(chunks - chunks // 2)

    scale = HEAD_SIZE ** (-0.5)
    high[...] = jnp.full_like(high, masked_score)
    total[...] = jnp.zeros_like(total)
    accum[...] = jnp.zeros_like(accum)
    own_pos = lax.broadcasted_iota(jnp.int32, (block, 1), 0)
    own_start = start - b * block
    key_lane = lax.broadcasted_iota(jnp.int32, (1, block), 1)

    def attend(d):
        key_pos = key_lane - d * block
        keep = (key_pos >= own_start) & (key_pos <= own_pos)

        def one(j, _):
            cols = pl.ds(pl.multiple_of(j * HEAD_SIZE, HEAD_SIZE), HEAD_SIZE)
            scores = lax.dot_general(
                query[:, cols], kv[d, :, :HEAD_SIZE], (((1,), (1,)), ((), ())),
                preferred_element_type=f32,
            ) * scale
            scores = jnp.where(keep, scores, masked_score)
            old = high[j]
            new = jnp.maximum(old, jnp.max(scores, axis=1, keepdims=True))
            fading = jnp.exp(old - new)
            probs = jnp.where(keep, jnp.exp(scores - new), 0.0)
            total[j] = total[j] * fading + jnp.sum(probs, axis=1, keepdims=True)
            update = jnp.dot(probs.astype(bf16), kv[d, :, HEAD_SIZE:], preferred_element_type=f32)
            accum[:, cols] = accum[:, cols] * fading + update
            high[j] = new
            return 0

        lax.fori_loop(0, q_heads, one, 0)

    for c in range(chunks):
        if c >= chunks // 2:
            cross_own(c)
        for s in range(1, steps):
            if (c, s) in line_events:
                line_step(c, s)
            cross_step(c, s)
        if c == 0:
            attend(0)
    early = min(2, chunks)
    for c in range(early):
        balance(c)

    def earlier(d, _):
        @pl.when(b >= d)
        def _():
            remote(kv.at[d], kv.at[d], kv_send.at[d], kv_recv.at[d], at_blk(lax.rem(b + 1, n))).wait_recv()
            attend(d)
        return 0

    lax.fori_loop(1, reach + 1, earlier, 0)

    for g in range(heads):
        rows = slice(g * tokens_own, (g + 1) * tokens_own)
        for j in range(q_heads):
            cols = slice(j * HEAD_SIZE, (j + 1) * HEAD_SIZE)
            mixed[g % 2, g // 2, :, cols] = (accum[rows, cols] / total[j, rows]).astype(bf16)

    tile = min(512, chunk_cols)

    def weight_tile(c, cols):
        right = w_proj[c, :, :, cols]
        if rows_out % 16:
            return right.astype(f32).reshape(n * rows_out, tile).astype(bf16)
        return right.reshape(n * rows_out, tile)

    def near_copy(c):
        return remote(near_send.at[c], near_recv.at[c], near_ss.at[c], near_rs.at[c], at_head(mate))

    def far_copy(c, o):
        other = lax.rem(y + o, outer)
        return remote(far_send.at[c, o], far_recv.at[c, o], far_ss.at[c, o], far_rs.at[c, o],
                      at_head(other * 2 + core))

    def project_out(c):
        keep_out[c].wait()
        await_crossed(c)

        def theirs(k, _):
            cols = pl.ds(pl.multiple_of(k * tile, tile), tile)
            left = mixed[1 - core].reshape(outer * tokens_own, q_cols)
            term = jnp.dot(left, weight_tile(c, cols), preferred_element_type=f32)
            near_send[c, :, :, cols] = term.astype(bf16).reshape(outer, tokens_own, tile)
            return 0

        def ours(k, _):
            cols = pl.ds(pl.multiple_of(k * tile, tile), tile)
            left = mixed[core].reshape(outer * tokens_own, q_cols)
            term = jnp.dot(left, weight_tile(c, cols), preferred_element_type=f32)
            part[c, :, :, cols] = term.reshape(outer, tokens_own, tile)
            return 0

        lax.fori_loop(0, chunk_cols // tile, theirs, 0)
        near_copy(c).start()
        lax.fori_loop(0, chunk_cols // tile, ours, 0)
        near_copy(c).wait_recv()
        for o in range(1, outer):
            other = lax.rem(y + o, outer)
            far_send[c, o] = (part[c, other] + near_recv[c, other].astype(f32)).astype(bf16)
            far_copy(c, o).start()

    def finish(c):
        result = part[c, y] + near_recv[c, y].astype(f32)
        for o in range(1, outer):
            far_copy(c, o).wait_recv()
            result = result + far_recv[c, o].astype(f32)
        out_ref[:, c * chunk_cols:(c + 1) * chunk_cols] = result.astype(bf16)

    for c in range(chunks):
        project_out(c)
        if early <= c + 1 < chunks:
            balance(c + 1)
        if c > 0:
            finish(c - 1)
    finish(chunks - 1)

    def drain(c):
        def one(row, _):
            @pl.when((row <= z) & (z < steps - 1))
            def _():
                send_copy(c, UP, row, False).wait_send()

            @pl.when((row >= z) & (z > 0))
            def _():
                send_copy(c, DOWN, row, False).wait_send()

            @pl.when(crosses(c, row))
            def _():
                send_copy(c, ACROSS, row, False).wait_send()
            return 0

        lax.fori_loop(0, steps, one, 0)

    for c in range(KEYVAL, chunks):
        drain(c)
    for c in range(chunks):
        @pl.when(twin < steps)
        def _():
            side_copy(c).wait_send()

        near_copy(c).wait_send()
        for o in range(1, outer):
            far_copy(c, o).wait_send()
    for copy in act_copies:
        copy.wait_send()

    def kv_drain(d, _):
        @pl.when(b + d < n)
        def _():
            kv_copy(d).wait_send()
        return 0

    lax.fori_loop(1, reach + 1, kv_drain, 0)


def on_device(tokens, w_query, key_value_weight, w_out, doc_lengths):
    n = lax.axis_size("blk")
    heads = lax.axis_size("heads")
    chunks = CHUNKS
    outer = heads // 2
    steps = n // LINE
    own, width = tokens.shape
    block = own * heads
    rows_in, q_cols = w_query.shape
    kv_cols = 2 * key_value_weight.shape[2]
    rows_out = w_out.shape[0]
    chunk_cols = width // chunks
    q_heads = q_cols // HEAD_SIZE
    reach = n // 4
    half = HEAD_SIZE // 2
    freqs = np.power(rope_base, -2.0 * np.arange(half) / HEAD_SIZE).astype(np.float32)
    freqs = jnp.asarray(np.concatenate([freqs, freqs])[None, :])
    bf16, f32 = jnp.bfloat16, jnp.float32
    dma = pltpu.SemaphoreType.DMA
    return pl.pallas_call(
        functools.partial(layer_kernel, n, heads, chunks),
        out_shape=jax.ShapeDtypeStruct((own, width), bf16),
        in_specs=[
            pl.BlockSpec(memory_space=pltpu.VMEM),
            pl.BlockSpec(memory_space=pl.ANY),
            pl.BlockSpec(memory_space=pltpu.VMEM),
            pl.BlockSpec(memory_space=pl.ANY),
            pl.BlockSpec(memory_space=pltpu.SMEM),
            pl.BlockSpec(memory_space=pltpu.VMEM),
        ],
        out_specs=pl.BlockSpec(memory_space=pltpu.VMEM),
        scratch_shapes=[
            pltpu.VMEM((n * rows_in, q_cols), bf16),
            pltpu.VMEM((n * rows_in, kv_cols), bf16),
            pltpu.VMEM((chunks, n, rows_out, chunk_cols), bf16),
            pltpu.VMEM((heads, own, width), bf16),
            pltpu.VMEM((block, q_cols + kv_cols), f32),
            pltpu.VMEM((block, q_cols), bf16),
            pltpu.VMEM((reach + 1, block, kv_cols), bf16),
            pltpu.VMEM((q_heads, block, 1), f32),
            pltpu.VMEM((q_heads, block, 1), f32),
            pltpu.VMEM((block, q_cols), f32),
            pltpu.VMEM((2, outer, own, q_cols), bf16),
            pltpu.VMEM((2, block, HEAD_SIZE), f32),
            pltpu.VMEM((chunks, outer, own, chunk_cols), bf16),
            pltpu.VMEM((chunks, outer, own, chunk_cols), bf16),
            pltpu.VMEM((chunks, outer, own, chunk_cols), f32),
            pltpu.VMEM((chunks, outer, own, chunk_cols), bf16),
            pltpu.VMEM((chunks, outer, own, chunk_cols), bf16),
            dma((chunks + 1,)),
            dma((2, 3, steps)),
            dma((2, n)),
            dma((chunks, 3, steps)),
            dma((chunks, n)),
            dma((chunks,)),
            dma((2 * outer,)),
            dma((heads,)),
            dma((reach + 1,)),
            dma((reach + 1,)),
            dma((chunks,)),
            dma((chunks,)),
            dma((chunks, outer)),
            dma((chunks, outer)),
        ],
        compiler_params=pltpu.CompilerParams(
            collective_id=0, has_side_effects=True, vmem_limit_bytes=60 * 1024 * 1024
        ),
    )(tokens, w_query, key_value_weight, w_out, doc_lengths, freqs)


def solution(mesh):
    return jax.shard_map(
        on_device,
        mesh=mesh,
        in_specs=(
            P(("blk", "heads"), None),
            P("blk", "heads"),
            P("blk", None, "heads"),
            P(("heads", "blk"), None),
            P(),
        ),
        out_specs=P(("blk", "heads"), None),
        check_vma=False,
    )
```

profile of v0, /device:TPU:27, one launch (start us, length us, event | category | flops | bytes accessed | tf_op | source)
XLA Modules:
  0.0 143.7 jit_solution(10434222267317909547)
XLA Ops:
  0.0 141.4 %shard_map.64 = bf16[128,4096]{1,0:T(8,128)(2,1)} custom-call(bf16[128,4096]{1,0:T(8,128)(2,1)} %tok_ref.1, bf16[512,512]{1,0:T(8,128)(2,1)} %w_query_ref.1, bf16[512,2,128]{2,1,0:T(2,128)(2,1)} %w_keyval_ref.1, bf16[64,4096]{1,0:T(8,128)(2,1)} %w_out_ref.1, s32[16]{0:T(128)} %len_ref.1, f32[1,128]{1,0:T(1,128)} %constant.2.clone.freq_ref), custom_call_target="tpu_custom_call" | custom-call | tf_op jit(solution)/shard_map/pallas_call | solution.py:463
  141.4 2.3 %copy.8 = bf16[128,4096]{1,0:T(8,128)(2,1)} copy(bf16[128,4096]{1,0:T(8,128)(2,1)} %shard_map.64) | data formatting | bytes 2097152
where the time goes:
time: 144 us
  Pallas kernels  141 us (98%)
  local copies, waits for them, and re-layouts  2.29 us (2%)
    pallas_call x1, Pallas kernels, on_device(): pl.pallas_call(functools.partial(layer_kernel, n, heads, chunks), out_sha...  141 us

commit v1 on v0

v1 whole, which is shorter than its diff:
```python
import functools

import jax
import jax.numpy as jnp
import numpy as np
from jax import lax
from jax.experimental import pallas as pl
from jax.experimental.pallas import tpu as pltpu
from jax.sharding import PartitionSpec as P

HEAD_SIZE = 128
LINE = 2
Q_UNITS = 2
CHUNKS = 4

norm_epsilon = 1e-05
rope_base = 500000.0
masked_score = -1e30
MESH = pl.DeviceIdType.MESH
UP, DOWN = 0, 1


def layer_kernel(
    n, heads, chunks, q_units,
    tok_ref, w_query_ref, w_keyval_ref, w_out_ref, len_ref, freq_ref, out_ref,
    w_kv, w_q, w_proj, kv_stage, act_stage, acts, qkv, query, kv, high, total, accum, mixed, rope, osend, obuf,
    line_send, mate_send, recv, cross_send, local_sem, redis_send, redis_recv,
    act_send, act_recv, kv_send, kv_recv, mix_send, mix_recv, out_send, out_recv,
):
    f32, bf16 = jnp.float32, jnp.bfloat16
    b = lax.axis_index("blk")
    h = lax.axis_index("heads")
    steps = n // LINE
    z, x = b // LINE, b % LINE
    y, core = h // 2, h % 2
    group = 2 * y + x
    block_id = LINE * z + core
    apart = (x + core) % 2
    reach = n // 4
    own, width = tok_ref.shape
    rows_in = w_query_ref.shape[0]
    block = own * heads
    q_cols = query.shape[1]
    q_heads = q_cols // HEAD_SIZE
    unit_cols = q_cols // q_units
    unit_heads = q_heads // q_units
    col_width = width // heads
    chunk_cols = col_width // chunks
    half = width // 2
    first_out = 1 + q_units
    units = first_out + chunks

    def dev(x_, y_, z_, c_):
        return {"blk": LINE * z_ + x_, "heads": 2 * y_ + c_}

    mate = dev(x, y, z, 1 - core)

    def remote(src, dst, ss, rs, device):
        return pltpu.make_async_remote_copy(
            src_ref=src, dst_ref=dst, send_sem=ss, recv_sem=rs, device_id=device, device_id_type=MESH
        )

    barrier = pltpu.get_barrier_semaphore()
    for dx, dy, dc in [(i, j, k) for i in (0, 1) for j in (0, 1) for k in (0, 1) if i + j + k]:
        pl.semaphore_signal(
            barrier, inc=1, device_id=dev((x + dx) % 2, (y + dy) % 2, z, (core + dc) % 2), device_id_type=MESH
        )
    span = (reach + 1) // 2
    for d in range(1, span + 1):
        for c_ in (0, 1):
            @pl.when(z + d < steps)
            def _():
                pl.semaphore_signal(barrier, inc=1, device_id=dev(x, y, z + d, c_), device_id_type=MESH)

            @pl.when(z - d >= 0)
            def _():
                pl.semaphore_signal(barrier, inc=1, device_id=dev(x, y, z - d, c_), device_id_type=MESH)
    near = jnp.minimum(z, span) + jnp.minimum(steps - 1 - z, span)
    pl.semaphore_wait(barrier, 7 + 2 * near)

    def unit_ref(u, k, row):
        i = LINE * row + k
        if u == 0:
            return w_kv.at[pl.ds(pl.multiple_of(i * rows_in, rows_in), rows_in)]
        if u < first_out:
            return w_q.at[u - 1, pl.ds(pl.multiple_of(i * rows_in, rows_in), rows_in)]
        return w_proj.at[:, k, pl.ds(LINE * row, LINE), :, pl.ds((u - first_out) * chunk_cols, chunk_cols)]

    def line_copy(u, direction, row):
        ref = unit_ref(u, core, row)
        z_ = z + 1 if direction == UP else z - 1
        return remote(ref, ref, line_send.at[u, direction, row], recv.at[u, core, row], dev(x, y, z_, core))

    def mate_copy(u, row):
        ref = unit_ref(u, core, row)
        return remote(ref, ref, mate_send.at[u, row], recv.at[u, core, row], mate)

    def arrive(u, k, row):
        ref = unit_ref(u, k, row)
        remote(ref, ref, mate_send.at[u, 0], recv.at[u, k, row], mate).wait_recv()

    def query_cols(u):
        return w_query_ref.at[:, pl.ds((u - 1) * unit_cols, unit_cols)]

    def cross_copy(u):
        src = kv_stage if u == 0 else query_cols(u)
        return remote(src, unit_ref(u, x, z), cross_send.at[u], recv.at[u, x, z], dev(1 - x, y, z, 1 - core))

    def keep_query(u):
        return pltpu.make_async_copy(query_cols(u), unit_ref(u, core, z), local_sem.at[u])

    def own_start(u):
        @pl.when(z < steps - 1)
        def _():
            line_copy(u, UP, z).start()

        @pl.when(z > 0)
        def _():
            line_copy(u, DOWN, z).start()

        mate_copy(u, z).start()

    def redis_peers():
        return [(1 - x, y), (x, 1 - y), (1 - x, 1 - y)]

    def redis_copy(i, x_, y_):
        cols = pl.ds(pl.multiple_of((2 * y_ + x_) * col_width, col_width), col_width)
        return remote(
            w_out_ref.at[:, cols], w_proj.at[y, core, b], redis_send.at[i], redis_recv.at[group],
            dev(x_, y_, z, core),
        )

    def keep_out():
        cols = pl.ds(pl.multiple_of(group * col_width, col_width), col_width)
        return pltpu.make_async_copy(w_out_ref.at[:, cols], w_proj.at[y, core, b], local_sem.at[0])

    def own_wait(u):
        if u == 0:
            @pl.when(apart == 1)
            def _():
                arrive(u, core, z)
        elif u < first_out:
            @pl.when(apart == 1)
            def _():
                arrive(u, core, z)

            @pl.when(apart == 0)
            def _():
                keep_query(u).wait()
        elif u == first_out:
            keep_out().wait()
            for x_, y_ in redis_peers():
                ref = w_proj.at[y_, core, LINE * z + x_]
                remote(ref, ref, redis_send.at[0], redis_recv.at[2 * y_ + x_], mate).wait_recv()

    def line_step(u, s):
        @pl.when(z - s >= 0)
        def _():
            arrive(u, core, z - s)

            @pl.when(z < steps - 1)
            def _():
                line_copy(u, UP, z - s).start()

            mate_copy(u, z - s).start()

        @pl.when(z + s <= steps - 1)
        def _():
            arrive(u, core, z + s)

            @pl.when(z > 0)
            def _():
                line_copy(u, DOWN, z + s).start()

            mate_copy(u, z + s).start()

    def line_steps(u, low, high_):
        def one(s, _):
            line_step(u, s)
            return 0

        lax.fori_loop(low, high_, one, 0)

    inner = (z > 0) & (z < steps - 1)

    def inner_steps(u, low, high_):
        @pl.when(inner)
        def _():
            line_steps(u, low, high_)

    def outer_steps(u, low, high_):
        @pl.when(jnp.logical_not(inner))
        def _():
            line_steps(u, low, high_)

    def mate_wait(u):
        def one(row, _):
            arrive(u, 1 - core, row)
            return 0

        lax.fori_loop(0, steps, one, 0)

    own_kv = w_keyval_ref[...].reshape(rows_in, w_kv.shape[1])

    @pl.when(apart == 0)
    def _():
        w_kv[pl.ds(pl.multiple_of(b * rows_in, rows_in), rows_in), :] = own_kv
        own_start(0)
        for u in range(1, first_out):
            keep_query(u).start()

    @pl.when(apart == 1)
    def _():
        kv_stage[...] = own_kv
        for u in range(first_out):
            cross_copy(u).start()

    keep_out().start()

    values = tok_ref[...].astype(f32)
    normed = (
        values * lax.rsqrt(jnp.mean(values * values, axis=1, keepdims=True) + norm_epsilon)
    ).astype(bf16)
    act_stage[...] = normed

    @pl.when(apart == 0)
    def _():
        acts[h] = normed

    def act_ref(h_, f):
        return acts.at[h_, :, pl.ds(pl.multiple_of(f * half, half), half)]

    def act_copy(i, h_, f, device, src=None):
        src = act_ref(h_, f) if src is None else src
        return remote(src, act_ref(h_, f), act_send.at[i], act_recv.at[f, h_], device)

    def act_own(i, f, device):
        return act_copy(i, h, f, device, act_stage.at[:, pl.ds(f * half, half)])

    def act_wait(h_, f):
        remote(act_ref(h_, f), act_ref(h_, f), act_send.at[0], act_recv.at[f, h_], mate).wait_recv()

    act_copies = [
        act_own(0, 1, dev(x, 1 - y, z, x)),
        act_own(1, 0, dev(1 - x, y, z, x)),
        act_own(2, 0, dev(x, 1 - y, z, x)),
        act_own(3, 1, dev(1 - x, y, z, x)),
    ]
    act_mate = [act_own(4 + f, f, mate) for f in (0, 1)]
    for copy in act_copies:
        copy.start()

    @pl.when(apart == 1)
    def _():
        for copy in act_mate:
            copy.start()

    redis_copies = [redis_copy(i, x_, y_) for i, (x_, y_) in enumerate(redis_peers())]
    for copy in redis_copies:
        copy.start()

    relay_half = 1 - apart
    relay_y = apart * y + (1 - apart) * (1 - y)
    relay_to = dev(
        apart * x + (1 - apart) * (1 - x), apart * (1 - y) + (1 - apart) * y, z, core
    )
    relays = [act_copy(6 + c, 2 * relay_y + c, relay_half, relay_to) for c in (0, 1)]

    def relay():
        for c, copy in enumerate(relays):
            act_wait(2 * relay_y + c, relay_half)
            copy.start()

    def acts_wait():
        for h_ in range(heads):
            for f in (0, 1):
                mine = (apart == 0) & (h == h_)
                relayed = (relay_half == f) & (relay_y == h_ // 2)

                @pl.when(jnp.logical_not(mine | relayed))
                def _():
                    act_wait(h_, f)

    @pl.when(apart == 1)
    def _():
        own_wait(0)
        own_start(0)

    pos = block_id * block + lax.broadcasted_iota(jnp.int32, (block, 1), 0)
    start = jnp.zeros((block, 1), jnp.int32)
    end = jnp.int32(0)
    for i in range(len_ref.shape[0]):
        size = len_ref[i]
        end = end + size
        start = start + jnp.where(pos >= end, size, 0)
    angle = (pos - start).astype(f32) * freq_ref[...]
    lane = lax.broadcasted_iota(jnp.int32, (block, HEAD_SIZE), 1)
    rope[0] = jnp.cos(angle)
    rope[1] = jnp.where(lane < HEAD_SIZE // 2, -jnp.sin(angle), jnp.sin(angle))
    qkv[...] = jnp.zeros_like(qkv)

    own_wait(1)
    own_start(1)
    line_steps(0, 1, 2)
    relay()
    line_steps(0, 2, steps)
    for u in range(2, first_out):
        own_wait(u)
        own_start(u)
        line_steps(u - 1, 1, steps)
    last_in = first_out - 1
    line_steps(last_in, 1, 2)
    acts_wait()

    depth = min(1024, width)

    def project(weights, cols):
        def one(k, _):
            rows = pl.ds(pl.multiple_of(k * depth, depth), depth)
            left = acts[:, :, rows].reshape(block, depth)
            qkv[:, cols] += jnp.dot(left, weights[rows, :], preferred_element_type=f32)
            return 0

        lax.fori_loop(0, width // depth, one, 0)

    def rotated(first):
        v = qkv[:, first:first + HEAD_SIZE]
        return (v * rope[0] + pltpu.roll(v, HEAD_SIZE // 2, 1) * rope[1]).astype(bf16)

    def project_query(u):
        mate_wait(u)
        first = (u - 1) * unit_cols
        project(w_q.at[u - 1], slice(first, first + unit_cols))
        for j in range(first // HEAD_SIZE, (first + unit_cols) // HEAD_SIZE):
            query[:, j * HEAD_SIZE:(j + 1) * HEAD_SIZE] = rotated(j * HEAD_SIZE)

    def kv_copy(d):
        to = block_id + d
        return remote(
            kv.at[0], kv.at[d], kv_send.at[d], kv_recv.at[d], dev(x, y, to // LINE, to % LINE)
        )

    def kv_start(d, _):
        @pl.when(block_id + d < n)
        def _():
            kv_copy(d).start()
        return 0

    own_pos = lax.broadcasted_iota(jnp.int32, (block, 1), 0)
    own_start_pos = start - block_id * block
    key_lane = lax.broadcasted_iota(jnp.int32, (1, block), 1)
    scale = HEAD_SIZE ** (-0.5) * float(np.log2(np.e))

    def attend_own(u):
        def one(j, _):
            cols = pl.ds(pl.multiple_of(j * HEAD_SIZE, HEAD_SIZE), HEAD_SIZE)
            keep = (key_lane >= own_start_pos) & (key_lane <= own_pos)
            scores = lax.dot_general(
                query[:, cols], kv[0, :, :HEAD_SIZE], (((1,), (1,)), ((), ())),
                preferred_element_type=f32,
            )
            scores = jnp.where(keep, scores, masked_score)
            new = jnp.max(scores, axis=1, keepdims=True)
            probs = jnp.exp2((scores - new) * scale)
            high[j] = new
            total[j] = jnp.sum(probs, axis=1, keepdims=True)
            accum[:, cols] = jnp.dot(probs.astype(bf16), kv[0, :, HEAD_SIZE:], preferred_element_type=f32)
            return 0

        lax.fori_loop((u - 1) * unit_heads, u * unit_heads, one, 0)

    def attend_earlier(u, d):
        keep = key_lane - d * block >= own_start_pos

        def one(j, _):
            cols = pl.ds(pl.multiple_of(j * HEAD_SIZE, HEAD_SIZE), HEAD_SIZE)
            scores = lax.dot_general(
                query[:, cols], kv[d, :, :HEAD_SIZE], (((1,), (1,)), ((), ())),
                preferred_element_type=f32,
            )
            scores = jnp.where(keep, scores, masked_score)
            old = high[j]
            new = jnp.maximum(old, jnp.max(scores, axis=1, keepdims=True))
            fading = jnp.exp2((old - new) * scale)
            probs = jnp.exp2((scores - new) * scale)
            total[j] = total[j] * fading + jnp.sum(probs, axis=1, keepdims=True)
            update = jnp.dot(probs.astype(bf16), kv[d, :, HEAD_SIZE:], preferred_element_type=f32)
            accum[:, cols] = accum[:, cols] * fading + update
            high[j] = new
            return 0

        lax.fori_loop((u - 1) * unit_heads, u * unit_heads, one, 0)

    def mix_cols(u):
        return pl.ds((u - 1) * unit_cols, unit_cols)

    def mix_copy(u, i, x_, y_):
        ref = mixed.at[group, :, mix_cols(u)]
        return remote(ref, ref, mix_send.at[u - 1, i], mix_recv.at[u - 1, group], dev(x_, y_, z, core))

    def finish_heads(u, first):
        def one(d, _):
            @pl.when(block_id >= d)
            def _():
                if first:
                    remote(kv.at[d], kv.at[d], kv_send.at[d], kv_recv.at[d], mate).wait_recv()
                attend_earlier(u, d)
            return 0

        lax.fori_loop(1, reach + 1, one, 0)
        for j in range((u - 1) * unit_heads, u * unit_heads):
            cols = slice(j * HEAD_SIZE, (j + 1) * HEAD_SIZE)
            mixed[group, :, cols] = (accum[:, cols] / total[j]).astype(bf16)
        for i, (x_, y_) in enumerate(redis_peers()):
            mix_copy(u, i, x_, y_).start()

    def mix_wait():
        for u in range(1, first_out):
            for x_, y_ in redis_peers():
                ref = mixed.at[2 * y_ + x_, :, mix_cols(u)]
                remote(ref, ref, mix_send.at[0, 0], mix_recv.at[u - 1, 2 * y_ + x_], mate).wait_recv()

    mate_wait(0)
    project(w_kv, slice(q_cols, q_cols + w_kv.shape[1]))
    kv[0, :, :HEAD_SIZE] = rotated(q_cols)
    kv[0, :, HEAD_SIZE:] = qkv[:, q_cols + HEAD_SIZE:].astype(bf16)
    lax.fori_loop(1, reach + 1, kv_start, 0)
    own_wait(first_out)
    own_start(first_out)
    inner_steps(last_in, 2, steps)
    for u in range(1, last_in):
        project_query(u)
        attend_own(u)
    outer_steps(last_in, 2, steps)
    own_start(first_out + 1)
    inner_steps(first_out, 1, steps)
    project_query(last_in)
    attend_own(last_in)
    own_start(first_out + 2)
    inner_steps(first_out + 1, 1, steps)
    finish_heads(1, True)
    for u in range(first_out + 2, units):
        if u + 1 < units:
            own_start(u + 1)
        inner_steps(u, 1, steps)
        if u == first_out + 2:
            for i in range(2, first_out):
                finish_heads(i, False)

    def out_copy(c, r):
        cols = pl.ds(pl.multiple_of(group * col_width + c * chunk_cols, chunk_cols), chunk_cols)
        return remote(
            osend.at[c, r], obuf.at[:, cols], out_send.at[c, r], out_recv.at[c, group],
            dev(core, r // 2, z, r % 2),
        )

    def away(r):
        return (apart == 1) | (h != r)

    def project_out(c):
        cols = slice(c * chunk_cols, (c + 1) * chunk_cols)
        result = None
        for g in range(heads):
            right = w_proj[g // 2, g % 2, :, :, cols]
            if right.shape[1] % 16:
                right = right.astype(f32).reshape(-1, chunk_cols).astype(bf16)
            else:
                right = right.reshape(-1, chunk_cols)
            term = jnp.dot(mixed[g], right, preferred_element_type=f32)
            result = term if result is None else result + term
        osend[c] = result.astype(bf16).reshape(heads, own, chunk_cols)
        for r in range(heads):
            @pl.when(away(r))
            def _():
                out_copy(c, r).start()

        @pl.when(apart == 0)
        def _():
            at = pl.ds(pl.multiple_of(group * col_width + c * chunk_cols, chunk_cols), chunk_cols)
            obuf[:, at] = osend[c, h]

    for c in range(chunks):
        outer_steps(first_out + c, 1, steps)
        mate_wait(first_out + c)
        if c == 0:
            mix_wait()
        project_out(c)

    for c in range(chunks):
        for g in range(heads):
            @pl.when((apart == 1) | (group != g))
            def _():
                first = g * col_width + c * chunk_cols
                ref = obuf.at[:, pl.ds(first, chunk_cols)]
                remote(ref, ref, out_send.at[0, 0], out_recv.at[c, g], mate).wait_recv()
    out_ref[...] = obuf[...]

    for u in range(units):
        def one(row, _):
            @pl.when((row <= z) & (z < steps - 1))
            def _():
                line_copy(u, UP, row).wait_send()

            @pl.when((row >= z) & (z > 0))
            def _():
                line_copy(u, DOWN, row).wait_send()

            mate_copy(u, row).wait_send()
            return 0

        lax.fori_loop(0, steps, one, 0)

    @pl.when(apart == 1)
    def _():
        for u in range(first_out):
            cross_copy(u).wait_send()
        for copy in act_mate:
            copy.wait_send()

    for copy in act_copies + relays + redis_copies:
        copy.wait_send()

    def kv_drain(d, _):
        @pl.when(block_id + d < n)
        def _():
            kv_copy(d).wait_send()
        return 0

    lax.fori_loop(1, reach + 1, kv_drain, 0)
    for u in range(1, first_out):
        for i, (x_, y_) in enumerate(redis_peers()):
            mix_copy(u, i, x_, y_).wait_send()
    for c in range(chunks):
        for r in range(heads):
            @pl.when(away(r))
            def _():
                out_copy(c, r).wait_send()


def on_device(tokens, w_query, key_value_weight, w_out, doc_lengths):
    n = lax.axis_size("blk")
    heads = lax.axis_size("heads")
    assert heads == 4
    chunks, q_units = CHUNKS, Q_UNITS
    steps = n // LINE
    own, width = tokens.shape
    block = own * heads
    rows_in, q_cols = w_query.shape
    kv_cols = 2 * key_value_weight.shape[2]
    rows_out = w_out.shape[0]
    col_width = width // heads
    chunk_cols = col_width // chunks
    q_heads = q_cols // HEAD_SIZE
    reach = n // 4
    units = 1 + q_units + chunks
    half = HEAD_SIZE // 2
    freqs = np.power(rope_base, -2.0 * np.arange(half) / HEAD_SIZE).astype(np.float32)
    freqs = jnp.asarray(np.concatenate([freqs, freqs])[None, :])
    bf16, f32 = jnp.bfloat16, jnp.float32
    dma = pltpu.SemaphoreType.DMA
    return pl.pallas_call(
        functools.partial(layer_kernel, n, heads, chunks, q_units),
        out_shape=jax.ShapeDtypeStruct((own, width), bf16),
        in_specs=[
            pl.BlockSpec(memory_space=pltpu.VMEM),
            pl.BlockSpec(memory_space=pl.ANY),
            pl.BlockSpec(memory_space=pltpu.VMEM),
            pl.BlockSpec(memory_space=pl.ANY),
            pl.BlockSpec(memory_space=pltpu.SMEM),
            pl.BlockSpec(memory_space=pltpu.VMEM),
        ],
        out_specs=pl.BlockSpec(memory_space=pltpu.VMEM),
        scratch_shapes=[
            pltpu.VMEM((n * rows_in, kv_cols), bf16),
            pltpu.VMEM((q_units, n * rows_in, q_cols // q_units), bf16),
            pltpu.VMEM((2, 2, n, rows_out, col_width), bf16),
            pltpu.VMEM((rows_in, kv_cols), bf16),
            pltpu.VMEM((own, width), bf16),
            pltpu.VMEM((heads, own, width), bf16),
            pltpu.VMEM((block, q_cols + kv_cols), f32),
            pltpu.VMEM((block, q_cols), bf16),
            pltpu.VMEM((reach + 1, block, kv_cols), bf16),
            pltpu.VMEM((q_heads, block, 1), f32),
            pltpu.VMEM((q_heads, block, 1), f32),
            pltpu.VMEM((block, q_cols), f32),
            pltpu.VMEM((heads, block, q_cols), bf16),
            pltpu.VMEM((2, block, HEAD_SIZE), f32),
            pltpu.VMEM((chunks, heads, own, chunk_cols), bf16),
            pltpu.VMEM((own, width), bf16),
            dma((units, 2, steps)),
            dma((units, steps)),
            dma((units, 2, steps)),
            dma((1 + q_units,)),
            dma((1 + q_units,)),
            dma((3,)),
            dma((heads,)),
            dma((8,)),
            dma((2, heads)),
            dma((reach + 1,)),
            dma((reach + 1,)),
            dma((q_units, 3)),
            dma((q_units, heads)),
            dma((chunks, heads)),
            dma((chunks, heads)),
        ],
        compiler_params=pltpu.CompilerParams(
            collective_id=0, has_side_effects=True, vmem_limit_bytes=60 * 1024 * 1024
        ),
    )(tokens, w_query, key_value_weight, w_out, doc_lengths, freqs)


def solution(mesh):
    return jax.shard_map(
        on_device,
        mesh=mesh,
        in_specs=(
            P(("blk", "heads"), None),
            P("blk", "heads"),
            P("blk", None, "heads"),
            P(("heads", "blk"), None),
            P(),
        ),
        out_specs=P(("blk", "heads"), None),
        check_vma=False,
    )
```

time: 144 us -> 133 us (0.924); the launches traced: 144 us -> 130 us
  Pallas kernels: 141 us -> 128 us
    pallas_call x1, Pallas kernels: 141 us -> 128 us  [on_device(): pl.pallas_call(functools.partial(layer_kernel, n, heads, chunks, q_units)...]
where the time goes in v1:
time: 133 us; the launch traced here: 130 us
  Pallas kernels  128 us (96%)
  local copies, waits for them, and re-layouts  2.29 us (2%)
    pallas_call x1, Pallas kernels, on_device(): pl.pallas_call(functools.partial(layer_kernel, n, heads, chunks, q_units)...  128 us

profile of v1, /device:TPU:27, one launch (start us, length us, event | category | flops | bytes accessed | tf_op | source)
XLA Modules:
  0.0 130.3 jit_solution(9899639680565243788)
XLA Ops:
  0.0 128.0 %shard_map.64 = bf16[128,4096]{1,0:T(8,128)(2,1)} custom-call(bf16[128,4096]{1,0:T(8,128)(2,1)} %tok_ref.1, bf16[512,512]{1,0:T(8,128)(2,1)} %w_query_ref.1, bf16[512,2,128]{2,1,0:T(2,128)(2,1)} %w_keyval_ref.1, bf16[64,4096]{1,0:T(8,128)(2,1)} %w_out_ref.1, s32[16]{0:T(128)} %len_ref.1, f32[1,128]{1,0:T(1,128)} %constant.2.clone.freq_ref), custom_call_target="tpu_custom_call" | custom-call | tf_op jit(solution)/shard_map/pallas_call | solution.py:561
  128.1 2.3 %copy.8 = bf16[128,4096]{1,0:T(8,128)(2,1)} copy(bf16[128,4096]{1,0:T(8,128)(2,1)} %shard_map.64) | data formatting | bytes 2097152

commit v2 on v1

--- a/solution.py
+++ b/solution.py
@@ -11,7 +11,8 @@
 HEAD_SIZE = 128
 LINE = 2
 Q_UNITS = 2
-CHUNKS = 4
+OUT_PARTS = (2, 2, 2, 1, 1)
+LEFT_PARTS = (5, 8)
 
 norm_epsilon = 1e-05
 rope_base = 500000.0
@@ -21,11 +22,11 @@
 
 
 def layer_kernel(
-    n, heads, chunks, q_units,
+    n, heads, out_cols, q_units,
     tok_ref, w_query_ref, w_keyval_ref, w_out_ref, len_ref, freq_ref, out_ref,
     w_kv, w_q, w_proj, kv_stage, act_stage, acts, qkv, query, kv, high, total, accum, mixed, rope, osend, obuf,
     line_send, mate_send, recv, cross_send, local_sem, redis_send, redis_recv,
-    act_send, act_recv, kv_send, kv_recv, mix_send, mix_recv, out_send, out_recv,
+    act_send, act_recv, kv_send, kv_recv, kv_pass_send, mix_send, mix_recv, out_send, out_recv,
 ):
     f32, bf16 = jnp.float32, jnp.bfloat16
     b = lax.axis_index("blk")
@@ -45,8 +46,9 @@
     unit_cols = q_cols // q_units
     unit_heads = q_heads // q_units
     col_width = width // heads
-    chunk_cols = col_width // chunks
-    half = width // 2
+    chunks = len(out_cols)
+    out_first = [sum(out_cols[:c]) for c in range(chunks)]
+    left = width * LEFT_PARTS[0] // LEFT_PARTS[1]
     first_out = 1 + q_units
     units = first_out + chunks
 
@@ -84,7 +86,7 @@
             return w_kv.at[pl.ds(pl.multiple_of(i * rows_in, rows_in), rows_in)]
         if u < first_out:
             return w_q.at[u - 1, pl.ds(pl.multiple_of(i * rows_in, rows_in), rows_in)]
-        return w_proj.at[:, k, pl.ds(LINE * row, LINE), :, pl.ds((u - first_out) * chunk_cols, chunk_cols)]
+        return w_proj.at[:, k, pl.ds(LINE * row, LINE), :, pl.ds(out_first[u - first_out], out_cols[u - first_out])]
 
     def line_copy(u, direction, row):
         ref = unit_ref(u, core, row)
@@ -212,7 +214,7 @@
     @pl.when(apart == 1)
     def _():
         kv_stage[...] = own_kv
-        for u in range(first_out):
+        for u in range(2):
             cross_copy(u).start()
 
     keep_out().start()
@@ -227,15 +229,17 @@
     def _():
         acts[h] = normed
 
+    act_cols = [(0, left), (left, width - left)]
+
     def act_ref(h_, f):
-        return acts.at[h_, :, pl.ds(pl.multiple_of(f * half, half), half)]
+        return acts.at[h_, :, pl.ds(*act_cols[f])]
 
     def act_copy(i, h_, f, device, src=None):
         src = act_ref(h_, f) if src is None else src
         return remote(src, act_ref(h_, f), act_send.at[i], act_recv.at[f, h_], device)
 
     def act_own(i, f, device):
-        return act_copy(i, h, f, device, act_stage.at[:, pl.ds(f * half, half)])
+        return act_copy(i, h, f, device, act_stage.at[:, pl.ds(*act_cols[f])])
 
     def act_wait(h_, f):
         remote(act_ref(h_, f), act_ref(h_, f), act_send.at[0], act_recv.at[f, h_], mate).wait_recv()
@@ -247,35 +251,39 @@
         act_own(3, 1, dev(1 - x, y, z, x)),
     ]
     act_mate = [act_own(4 + f, f, mate) for f in (0, 1)]
-    for copy in act_copies:
-        copy.start()
+    act_copies[0].start()
+    act_copies[1].start()
 
     @pl.when(apart == 1)
     def _():
+        for u in range(2, first_out):
+            cross_copy(u).start()
         for copy in act_mate:
             copy.start()
 
+    act_copies[2].start()
+    act_copies[3].start()
     redis_copies = [redis_copy(i, x_, y_) for i, (x_, y_) in enumerate(redis_peers())]
-    for copy in redis_copies:
-        copy.start()
-
-    relay_half = 1 - apart
+
     relay_y = apart * y + (1 - apart) * (1 - y)
-    relay_to = dev(
-        apart * x + (1 - apart) * (1 - x), apart * (1 - y) + (1 - apart) * y, z, core
-    )
-    relays = [act_copy(6 + c, 2 * relay_y + c, relay_half, relay_to) for c in (0, 1)]
-
-    def relay():
-        for c, copy in enumerate(relays):
-            act_wait(2 * relay_y + c, relay_half)
-            copy.start()
+
+    def relay_copy(i, f):
+        c = core if i == 0 else 1 - core
+        to = dev(x, 1 - y, z, core) if f == 0 else dev(1 - x, y, z, core)
+        return act_copy(6 + i, 2 * relay_y + c, f, to)
+
+    def relay(i):
+        for f in (0, 1):
+            @pl.when(apart == 1 - f)
+            def _():
+                act_wait(2 * relay_y + (core if i == 0 else 1 - core), f)
+                relay_copy(i, f).start()
 
     def acts_wait():
         for h_ in range(heads):
             for f in (0, 1):
                 mine = (apart == 0) & (h == h_)
-                relayed = (relay_half == f) & (relay_y == h_ // 2)
+                relayed = (apart == 1 - f) & (relay_y == h_ // 2)
 
                 @pl.when(jnp.logical_not(mine | relayed))
                 def _():
@@ -302,14 +310,32 @@
     own_wait(1)
     own_start(1)
     line_steps(0, 1, 2)
-    relay()
+    relay(0)
     line_steps(0, 2, steps)
-    for u in range(2, first_out):
-        own_wait(u)
-        own_start(u)
-        line_steps(u - 1, 1, steps)
+    relay(1)
+    for copy in redis_copies:
+        copy.start()
     last_in = first_out - 1
-    line_steps(last_in, 1, 2)
+
+    @pl.when(inner)
+    def _():
+        for u in range(2, first_out):
+            line_steps(u - 1, 1, steps)
+            own_wait(u)
+            own_start(u)
+        line_steps(last_in, 1, 2)
+
+    @pl.when(jnp.logical_not(inner))
+    def _():
+        for u in range(2, first_out):
+            own_wait(u)
+            own_start(u)
+
+    for d in range(1, reach + 1):
+        @pl.when(block_id < d)
+        def _():
+            kv[d] = jnp.zeros_like(kv[d])
+
     acts_wait()
 
     depth = min(1024, width)
@@ -334,17 +360,59 @@
         for j in range(first // HEAD_SIZE, (first + unit_cols) // HEAD_SIZE):
             query[:, j * HEAD_SIZE:(j + 1) * HEAD_SIZE] = rotated(j * HEAD_SIZE)
 
-    def kv_copy(d):
-        to = block_id + d
+    def kv_copy(k):
         return remote(
-            kv.at[0], kv.at[d], kv_send.at[d], kv_recv.at[d], dev(x, y, to // LINE, to % LINE)
+            kv.at[0], kv.at[2 * k], kv_send.at[2 * k], kv_recv.at[2 * k], dev(x, y, z + k, core)
         )
 
-    def kv_start(d, _):
-        @pl.when(block_id + d < n)
-        def _():
-            kv_copy(d).start()
-        return 0
+    kv_mate = remote(kv.at[0], kv.at[1], kv_send.at[1], kv_recv.at[1], mate)
+
+    def kv_pass_copy(k):
+        to = 2 * k + 1 - 2 * core
+        return remote(kv.at[2 * k], kv.at[to], kv_pass_send.at[2 * k], kv_recv.at[to], mate)
+
+    def kv_passes(k):
+        return (z >= k) & (2 * k + 1 - 2 * core <= reach)
+
+    def kv_each(low, high_, body):
+        def one(k, _):
+            body(k)
+            return 0
+
+        lax.fori_loop(low, high_, one, 0)
+
+    def kv_start():
+        @pl.when(core == 0)
+        def _():
+            kv_mate.start()
+
+        def one(k):
+            @pl.when(z + k < steps)
+            def _():
+                kv_copy(k).start()
+
+        kv_each(1, reach // 2 + 1, one)
+
+    def kv_wait(d):
+        remote(kv.at[d], kv.at[d], kv_send.at[d], kv_recv.at[d], mate).wait_recv()
+
+    def kv_ready():
+        def even(k):
+            @pl.when(z >= k)
+            def _():
+                kv_wait(2 * k)
+
+            @pl.when(kv_passes(k))
+            def _():
+                kv_pass_copy(k).start()
+
+        def odd(k):
+            @pl.when(block_id >= 2 * k + 1)
+            def _():
+                kv_wait(2 * k + 1)
+
+        kv_each(1, reach // 2 + 1, even)
+        kv_each(0, reach // 2, odd)
 
     own_pos = lax.broadcasted_iota(jnp.int32, (block, 1), 0)
     own_start_pos = start - block_id * block
@@ -391,6 +459,39 @@
 
         lax.fori_loop((u - 1) * unit_heads, u * unit_heads, one, 0)
 
+    def attend_tiles(u):
+        tile = block // 4
+
+        def one(j, _):
+            cols = pl.ds(pl.multiple_of(j * HEAD_SIZE, HEAD_SIZE), HEAD_SIZE)
+            for i in range(4):
+                rows = slice(i * tile, (i + 1) * tile)
+                spans = [(0, 0, (i + 1) * tile)]
+                spans += [(d, 0, block) for d in range(1, reach)]
+                spans += [(reach, i * tile, block)]
+                parts = []
+                for d, low, high_ in spans:
+                    scores = lax.dot_general(
+                        query[rows, cols], kv[d, low:high_, :HEAD_SIZE], (((1,), (1,)), ((), ())),
+                        preferred_element_type=f32,
+                    )
+                    key_pos = low - d * block + lax.broadcasted_iota(jnp.int32, (1, high_ - low), 1)
+                    keep = key_pos >= own_start_pos[rows]
+                    if d == 0:
+                        keep = keep & (key_pos <= own_pos[rows])
+                    parts.append(jnp.where(keep, scores, masked_score))
+                top = functools.reduce(jnp.maximum, [jnp.max(p, axis=1, keepdims=True) for p in parts])
+                probs = [jnp.exp2((p - top) * scale) for p in parts]
+                denom = sum(jnp.sum(p, axis=1, keepdims=True) for p in probs)
+                result = sum(
+                    jnp.dot(p.astype(bf16), kv[d, low:high_, HEAD_SIZE:], preferred_element_type=f32)
+                    for p, (d, low, high_) in zip(probs, spans)
+                )
+                mixed[group, rows, cols] = (result / denom).astype(bf16)
+            return 0
+
+        lax.fori_loop((u - 1) * unit_heads, u * unit_heads, one, 0)
+
     def mix_cols(u):
         return pl.ds((u - 1) * unit_cols, unit_cols)
 
@@ -398,12 +499,19 @@
         ref = mixed.at[group, :, mix_cols(u)]
         return remote(ref, ref, mix_send.at[u - 1, i], mix_recv.at[u - 1, group], dev(x_, y_, z, core))
 
-    def finish_heads(u, first):
+    def attend(u):
+        if reach <= 2:
+            attend_tiles(u)
+        else:
+            attend_own(u)
+            finish_heads(u)
+        for i, (x_, y_) in enumerate(redis_peers()):
+            mix_copy(u, i, x_, y_).start()
+
+    def finish_heads(u):
         def one(d, _):
             @pl.when(block_id >= d)
             def _():
-                if first:
-                    remote(kv.at[d], kv.at[d], kv_send.at[d], kv_recv.at[d], mate).wait_recv()
                 attend_earlier(u, d)
             return 0
 
@@ -411,8 +519,6 @@
         for j in range((u - 1) * unit_heads, u * unit_heads):
             cols = slice(j * HEAD_SIZE, (j + 1) * HEAD_SIZE)
             mixed[group, :, cols] = (accum[:, cols] / total[j]).astype(bf16)
-        for i, (x_, y_) in enumerate(redis_peers()):
-            mix_copy(u, i, x_, y_).start()
 
     def mix_wait():
         for u in range(1, first_out):
@@ -424,33 +530,52 @@
     project(w_kv, slice(q_cols, q_cols + w_kv.shape[1]))
     kv[0, :, :HEAD_SIZE] = rotated(q_cols)
     kv[0, :, HEAD_SIZE:] = qkv[:, q_cols + HEAD_SIZE:].astype(bf16)
-    lax.fori_loop(1, reach + 1, kv_start, 0)
-    own_wait(first_out)
-    own_start(first_out)
+    kv_start()
+    for u in range(1, last_in):
+        outer_steps(u, 1, steps)
     inner_steps(last_in, 2, steps)
     for u in range(1, last_in):
         project_query(u)
-        attend_own(u)
-    outer_steps(last_in, 2, steps)
-    own_start(first_out + 1)
-    inner_steps(first_out, 1, steps)
-    project_query(last_in)
-    attend_own(last_in)
-    own_start(first_out + 2)
-    inner_steps(first_out + 1, 1, steps)
-    finish_heads(1, True)
-    for u in range(first_out + 2, units):
-        if u + 1 < units:
-            own_start(u + 1)
-        inner_steps(u, 1, steps)
-        if u == first_out + 2:
-            for i in range(2, first_out):
-                finish_heads(i, False)
+    own_wait(first_out)
+    for u in range(first_out, units):
+        own_start(u)
+
+    def inner_out(low, high_):
+        @pl.when(inner)
+        def _():
+            def one(s, _):
+                for u in range(first_out, units):
+                    line_step(u, s)
+                return 0
+
+            lax.fori_loop(low, high_, one, 0)
+
+    @pl.when(inner)
+    def _():
+        project_query(last_in)
+
+    kv_ready()
+    for u in range(1, last_in):
+        attend(u)
+    outer_steps(last_in, 1, steps)
+
+    @pl.when(jnp.logical_not(inner))
+    def _():
+        project_query(last_in)
+
+    inner_out(1, 2)
+    attend(last_in)
+    inner_out(2, steps)
+
+    def out_at(g, c):
+        return pl.ds(pl.multiple_of(g * col_width + out_first[c], HEAD_SIZE), out_cols[c])
+
+    def out_part(r, c):
+        return osend.at[r, :, pl.ds(out_first[c], out_cols[c])]
 
     def out_copy(c, r):
-        cols = pl.ds(pl.multiple_of(group * col_width + c * chunk_cols, chunk_cols), chunk_cols)
         return remote(
-            osend.at[c, r], obuf.at[:, cols], out_send.at[c, r], out_recv.at[c, group],
+            out_part(r, c), obuf.at[:, out_at(group, c)], out_send.at[c, r], out_recv.at[c, group],
             dev(core, r // 2, z, r % 2),
         )
 
@@ -458,17 +583,17 @@
         return (apart == 1) | (h != r)
 
     def project_out(c):
-        cols = slice(c * chunk_cols, (c + 1) * chunk_cols)
+        cols = slice(out_first[c], out_first[c] + out_cols[c])
         result = None
         for g in range(heads):
             right = w_proj[g // 2, g % 2, :, :, cols]
             if right.shape[1] % 16:
-                right = right.astype(f32).reshape(-1, chunk_cols).astype(bf16)
+                right = right.astype(f32).reshape(-1, out_cols[c]).astype(bf16)
             else:
-                right = right.reshape(-1, chunk_cols)
+                right = right.reshape(-1, out_cols[c])
             term = jnp.dot(mixed[g], right, preferred_element_type=f32)
             result = term if result is None else result + term
-        osend[c] = result.astype(bf16).reshape(heads, own, chunk_cols)
+        osend[:, :, cols] = result.astype(bf16).reshape(heads, own, out_cols[c])
         for r in range(heads):
             @pl.when(away(r))
             def _():
@@ -476,8 +601,7 @@
 
         @pl.when(apart == 0)
         def _():
-            at = pl.ds(pl.multiple_of(group * col_width + c * chunk_cols, chunk_cols), chunk_cols)
-            obuf[:, at] = osend[c, h]
+            obuf[:, out_at(group, c)] = osend[h, :, cols]
 
     for c in range(chunks):
         outer_steps(first_out + c, 1, steps)
@@ -490,8 +614,7 @@
         for g in range(heads):
             @pl.when((apart == 1) | (group != g))
             def _():
-                first = g * col_width + c * chunk_cols
-                ref = obuf.at[:, pl.ds(first, chunk_cols)]
+                ref = obuf.at[:, out_at(g, c)]
                 remote(ref, ref, out_send.at[0, 0], out_recv.at[c, g], mate).wait_recv()
     out_ref[...] = obuf[...]
 
@@ -517,16 +640,28 @@
         for copy in act_mate:
             copy.wait_send()
 
-    for copy in act_copies + relays + redis_copies:
+    for copy in act_copies + redis_copies:
         copy.wait_send()
-
-    def kv_drain(d, _):
-        @pl.when(block_id + d < n)
-        def _():
-            kv_copy(d).wait_send()
-        return 0
-
-    lax.fori_loop(1, reach + 1, kv_drain, 0)
+    for f in (0, 1):
+        @pl.when(apart == 1 - f)
+        def _():
+            for i in (0, 1):
+                relay_copy(i, f).wait_send()
+
+    @pl.when(core == 0)
+    def _():
+        kv_mate.wait_send()
+
+    def kv_drain(k):
+        @pl.when(z + k < steps)
+        def _():
+            kv_copy(k).wait_send()
+
+        @pl.when(kv_passes(k))
+        def _():
+            kv_pass_copy(k).wait_send()
+
+    kv_each(1, reach // 2 + 1, kv_drain)
     for u in range(1, first_out):
         for i, (x_, y_) in enumerate(redis_peers()):
             mix_copy(u, i, x_, y_).wait_send()
@@ -541,7 +676,7 @@
     n = lax.axis_size("blk")
     heads = lax.axis_size("heads")
     assert heads == 4
-    chunks, q_units = CHUNKS, Q_UNITS
+    q_units, chunks = Q_UNITS, len(OUT_PARTS)
     steps = n // LINE
     own, width = tokens.shape
     block = own * heads
@@ -549,7 +684,7 @@
     kv_cols = 2 * key_value_weight.shape[2]
     rows_out = w_out.shape[0]
     col_width = width // heads
-    chunk_cols = col_width // chunks
+    out_cols = tuple(col_width * part // sum(OUT_PARTS) for part in OUT_PARTS)
     q_heads = q_cols // HEAD_SIZE
     reach = n // 4
     units = 1 + q_units + chunks
@@ -559,7 +694,7 @@
     bf16, f32 = jnp.bfloat16, jnp.float32
     dma = pltpu.SemaphoreType.DMA
     return pl.pallas_call(
-        functools.partial(layer_kernel, n, heads, chunks, q_units),
+        functools.partial(layer_kernel, n, heads, out_cols, q_units),
         out_shape=jax.ShapeDtypeStruct((own, width), bf16),
         in_specs=[
             pl.BlockSpec(memory_space=pltpu.VMEM),
@@ -585,7 +720,7 @@
             pltpu.VMEM((block, q_cols), f32),
             pltpu.VMEM((heads, block, q_cols), bf16),
             pltpu.VMEM((2, block, HEAD_SIZE), f32),
-            pltpu.VMEM((chunks, heads, own, chunk_cols), bf16),
+            pltpu.VMEM((heads, own, col_width), bf16),
             pltpu.VMEM((own, width), bf16),
             dma((units, 2, steps)),
             dma((units, steps)),
@@ -596,6 +731,7 @@
             dma((heads,)),
             dma((8,)),
             dma((2, heads)),
+            dma((reach + 1,)),
             dma((reach + 1,)),
             dma((reach + 1,)),
             dma((q_units, 3)),

time: 133 us -> 114 us (0.86); the launches traced: 130 us -> 113 us
  Pallas kernels: 128 us -> 110 us
    pallas_call x1, Pallas kernels: 128 us -> 110 us  [on_device(): pl.pallas_call(functools.partial(layer_kernel, n, heads, out_cols, q_unit...]
where the time goes in v2:
time: 114 us; the launch traced here: 113 us
  Pallas kernels  110 us (96%)
  local copies, waits for them, and re-layouts  2.29 us (2%)
    pallas_call x1, Pallas kernels, on_device(): pl.pallas_call(functools.partial(layer_kernel, n, heads, out_cols, q_unit...  110 us
    unnamed x1, local copies, waits for them, and re-layouts  2.29 us

profile of v2, /device:TPU:27, one launch (start us, length us, event | category | flops | bytes accessed | tf_op | source)
XLA Modules:
  0.0 112.7 jit_solution(7813238160456305241)
XLA Ops:
  0.0 110.4 %shard_map.64 = bf16[128,4096]{1,0:T(8,128)(2,1)} custom-call(bf16[128,4096]{1,0:T(8,128)(2,1)} %tok_ref.1, bf16[512,512]{1,0:T(8,128)(2,1)} %w_query_ref.1, bf16[512,2,128]{2,1,0:T(2,128)(2,1)} %w_keyval_ref.1, bf16[64,4096]{1,0:T(8,128)(2,1)} %w_out_ref.1, s32[16]{0:T(128)} %len_ref.1, f32[1,128]{1,0:T(1,128)} %constant.2.clone.freq_ref), custom_call_target="tpu_custom_call" | custom-call | tf_op jit(solution)/shard_map/pallas_call | solution.py:696
  110.4 2.3 %copy.8 = bf16[128,4096]{1,0:T(8,128)(2,1)} copy(bf16[128,4096]{1,0:T(8,128)(2,1)} %shard_map.64) | data formatting | bytes 2097152

commit v3 on v2

--- a/solution.py
+++ b/solution.py
@@ -11,7 +11,7 @@
 HEAD_SIZE = 128
 LINE = 2
 Q_UNITS = 2
-OUT_PARTS = (2, 2, 2, 1, 1)
+OUT_PARTS = (4, 2, 2)
 LEFT_PARTS = (5, 8)
 
 norm_epsilon = 1e-05
@@ -24,8 +24,8 @@
 def layer_kernel(
     n, heads, out_cols, q_units,
     tok_ref, w_query_ref, w_keyval_ref, w_out_ref, len_ref, freq_ref, out_ref,
-    w_kv, w_q, w_proj, kv_stage, act_stage, acts, qkv, query, kv, high, total, accum, mixed, rope, osend, obuf,
-    line_send, mate_send, recv, cross_send, local_sem, redis_send, redis_recv,
+    tok_buf, kv_raw, freq_buf, w_kv, w_q, w_proj, kv_stage, act_stage, acts, qkv, query, kv, high, total, accum, mixed, rope, osend, obuf,
+    line_send, mate_send, recv, cross_send, local_sem, load_sem, store_sem, redis_send, redis_recv,
     act_send, act_recv, kv_send, kv_recv, kv_pass_send, mix_send, mix_recv, out_send, out_recv,
 ):
     f32, bf16 = jnp.float32, jnp.bfloat16
@@ -78,7 +78,12 @@
             def _():
                 pl.semaphore_signal(barrier, inc=1, device_id=dev(x, y, z - d, c_), device_id_type=MESH)
     near = jnp.minimum(z, span) + jnp.minimum(steps - 1 - z, span)
-    pl.semaphore_wait(barrier, 7 + 2 * near)
+    loads = [
+        pltpu.make_async_copy(src, dst, load_sem.at[i])
+        for i, (src, dst) in enumerate([(w_keyval_ref, kv_raw), (tok_ref, tok_buf), (freq_ref, freq_buf)])
+    ]
+    for load in loads:
+        load.start()
 
     def unit_ref(u, k, row):
         i = LINE * row + k
@@ -91,7 +96,10 @@
     def line_copy(u, direction, row):
         ref = unit_ref(u, core, row)
         z_ = z + 1 if direction == UP else z - 1
-        return remote(ref, ref, line_send.at[u, direction, row], recv.at[u, core, row], dev(x, y, z_, core))
+        at = row
+        if direction == DOWN:
+            at = jnp.where(row == z, steps, row)
+        return remote(ref, ref, line_send.at[u, at], recv.at[u, core, row], dev(x, y, z_, core))
 
     def mate_copy(u, row):
         ref = unit_ref(u, core, row)
@@ -202,24 +210,25 @@
 
         lax.fori_loop(0, steps, one, 0)
 
-    own_kv = w_keyval_ref[...].reshape(rows_in, w_kv.shape[1])
-
     @pl.when(apart == 0)
     def _():
-        w_kv[pl.ds(pl.multiple_of(b * rows_in, rows_in), rows_in), :] = own_kv
-        own_start(0)
         for u in range(1, first_out):
             keep_query(u).start()
 
+    keep_out().start()
+    loads[0].wait()
+    own_kv = kv_raw[...].reshape(rows_in, w_kv.shape[1])
+
+    @pl.when(apart == 0)
+    def _():
+        w_kv[pl.ds(pl.multiple_of(b * rows_in, rows_in), rows_in), :] = own_kv
+
     @pl.when(apart == 1)
     def _():
         kv_stage[...] = own_kv
-        for u in range(2):
-            cross_copy(u).start()
-
-    keep_out().start()
-
-    values = tok_ref[...].astype(f32)
+
+    loads[1].wait()
+    values = tok_buf[...].astype(f32)
     normed = (
         values * lax.rsqrt(jnp.mean(values * values, axis=1, keepdims=True) + norm_epsilon)
     ).astype(bf16)
@@ -228,6 +237,19 @@
     @pl.when(apart == 0)
     def _():
         acts[h] = normed
+
+    pl.semaphore_wait(barrier, 7 + 2 * near)
+
+    @pl.when(apart == 0)
+    def _():
+        own_start(0)
+        own_wait(1)
+        own_start(1)
+
+    @pl.when(apart == 1)
+    def _():
+        for u in range(2):
+            cross_copy(u).start()
 
     act_cols = [(0, left), (left, width - left)]
 
@@ -252,17 +274,17 @@
     ]
     act_mate = [act_own(4 + f, f, mate) for f in (0, 1)]
     act_copies[0].start()
-    act_copies[1].start()
+    act_copies[2].start()
 
     @pl.when(apart == 1)
     def _():
+        act_copies[1].start()
         for u in range(2, first_out):
             cross_copy(u).start()
         for copy in act_mate:
             copy.start()
-
-    act_copies[2].start()
-    act_copies[3].start()
+        act_copies[3].start()
+
     redis_copies = [redis_copy(i, x_, y_) for i, (x_, y_) in enumerate(redis_peers())]
 
     relay_y = apart * y + (1 - apart) * (1 - y)
@@ -301,15 +323,25 @@
         size = len_ref[i]
         end = end + size
         start = start + jnp.where(pos >= end, size, 0)
-    angle = (pos - start).astype(f32) * freq_ref[...]
+    loads[2].wait()
+    angle = (pos - start).astype(f32) * freq_buf[...]
     lane = lax.broadcasted_iota(jnp.int32, (block, HEAD_SIZE), 1)
     rope[0] = jnp.cos(angle)
     rope[1] = jnp.where(lane < HEAD_SIZE // 2, -jnp.sin(angle), jnp.sin(angle))
     qkv[...] = jnp.zeros_like(qkv)
 
-    own_wait(1)
-    own_start(1)
+    @pl.when(apart == 1)
+    def _():
+        own_wait(1)
+        own_start(1)
+
     line_steps(0, 1, 2)
+
+    @pl.when(apart == 0)
+    def _():
+        act_copies[1].start()
+        act_copies[3].start()
+
     relay(0)
     line_steps(0, 2, steps)
     relay(1)
@@ -537,18 +569,12 @@
     for u in range(1, last_in):
         project_query(u)
     own_wait(first_out)
-    for u in range(first_out, units):
-        own_start(u)
-
-    def inner_out(low, high_):
-        @pl.when(inner)
-        def _():
-            def one(s, _):
-                for u in range(first_out, units):
-                    line_step(u, s)
-                return 0
-
-            lax.fori_loop(low, high_, one, 0)
+    own_start(first_out)
+
+    @pl.when(jnp.logical_not(inner))
+    def _():
+        for u in range(first_out + 1, units):
+            own_start(u)
 
     @pl.when(inner)
     def _():
@@ -563,9 +589,25 @@
     def _():
         project_query(last_in)
 
-    inner_out(1, 2)
+    @pl.when(inner)
+    def _():
+        line_step(first_out, 1)
+        for u in range(first_out + 1, units):
+            own_start(u)
+
     attend(last_in)
-    inner_out(2, steps)
+
+    @pl.when(inner)
+    def _():
+        def one(s, _):
+            line_step(first_out, s)
+            for u in range(first_out + 1, units):
+                line_step(u, s - 1)
+            return 0
+
+        lax.fori_loop(2, steps, one, 0)
+        for u in range(first_out + 1, units):
+            line_step(u, steps - 1)
 
     def out_at(g, c):
         return pl.ds(pl.multiple_of(g * col_width + out_first[c], HEAD_SIZE), out_cols[c])
@@ -603,73 +645,100 @@
         def _():
             obuf[:, out_at(group, c)] = osend[h, :, cols]
 
+    def drain_unit(u):
+        def one(row, _):
+            @pl.when((row <= z) & (z < steps - 1))
+            def _():
+                line_copy(u, UP, row).wait_send()
+
+            @pl.when((row >= z) & (z > 0))
+            def _():
+                line_copy(u, DOWN, row).wait_send()
+
+            mate_copy(u, row).wait_send()
+            return 0
+
+        lax.fori_loop(0, steps, one, 0)
+
+    def drain_in():
+        for u in range(first_out):
+            drain_unit(u)
+
+        @pl.when(apart == 1)
+        def _():
+            for u in range(first_out):
+                cross_copy(u).wait_send()
+            for copy in act_mate:
+                copy.wait_send()
+
+        for copy in act_copies + redis_copies:
+            copy.wait_send()
+        for f in (0, 1):
+            @pl.when(apart == 1 - f)
+            def _():
+                for i in (0, 1):
+                    relay_copy(i, f).wait_send()
+
+        @pl.when(core == 0)
+        def _():
+            kv_mate.wait_send()
+
+        def kv_drain(k):
+            @pl.when(z + k < steps)
+            def _():
+                kv_copy(k).wait_send()
+
+            @pl.when(kv_passes(k))
+            def _():
+                kv_pass_copy(k).wait_send()
+
+        kv_each(1, reach // 2 + 1, kv_drain)
+        for u in range(1, first_out):
+            for i, (x_, y_) in enumerate(redis_peers()):
+                mix_copy(u, i, x_, y_).wait_send()
+
+    def store_copy(c, g):
+        return pltpu.make_async_copy(
+            obuf.at[:, out_at(g, c)], out_ref.at[:, out_at(g, c)], store_sem.at[c, g]
+        )
+
+    def take_out(c):
+        for g in range(heads):
+            @pl.when((apart == 1) | (group != g))
+            def _():
+                ref = obuf.at[:, out_at(g, c)]
+                remote(ref, ref, out_send.at[0, 0], out_recv.at[c, g], mate).wait_recv()
+
+            store_copy(c, g).start()
+
+    def drain_out(c):
+        drain_unit(first_out + c)
+        for r in range(heads):
+            @pl.when(away(r))
+            def _():
+                out_copy(c, r).wait_send()
+
+        for g in range(heads):
+            store_copy(c, g).wait()
+
     for c in range(chunks):
         outer_steps(first_out + c, 1, steps)
         mate_wait(first_out + c)
         if c == 0:
             mix_wait()
         project_out(c)
-
-    for c in range(chunks):
-        for g in range(heads):
-            @pl.when((apart == 1) | (group != g))
-            def _():
-                ref = obuf.at[:, out_at(g, c)]
-                remote(ref, ref, out_send.at[0, 0], out_recv.at[c, g], mate).wait_recv()
-    out_ref[...] = obuf[...]
-
-    for u in range(units):
-        def one(row, _):
-            @pl.when((row <= z) & (z < steps - 1))
-            def _():
-                line_copy(u, UP, row).wait_send()
-
-            @pl.when((row >= z) & (z > 0))
-            def _():
-                line_copy(u, DOWN, row).wait_send()
-
-            mate_copy(u, row).wait_send()
-            return 0
-
-        lax.fori_loop(0, steps, one, 0)
-
-    @pl.when(apart == 1)
-    def _():
-        for u in range(first_out):
-            cross_copy(u).wait_send()
-        for copy in act_mate:
-            copy.wait_send()
-
-    for copy in act_copies + redis_copies:
-        copy.wait_send()
-    for f in (0, 1):
-        @pl.when(apart == 1 - f)
-        def _():
-            for i in (0, 1):
-                relay_copy(i, f).wait_send()
-
-    @pl.when(core == 0)
-    def _():
-        kv_mate.wait_send()
-
-    def kv_drain(k):
-        @pl.when(z + k < steps)
-        def _():
-            kv_copy(k).wait_send()
-
-        @pl.when(kv_passes(k))
-        def _():
-            kv_pass_copy(k).wait_send()
-
-    kv_each(1, reach // 2 + 1, kv_drain)
-    for u in range(1, first_out):
-        for i, (x_, y_) in enumerate(redis_peers()):
-            mix_copy(u, i, x_, y_).wait_send()
-    for c in range(chunks):
-        for r in range(heads):
-            @pl.when(away(r))
-            def _():
-                out_copy(c, r).wait_send()
+        if c == 0:
+            drain_in()
+        if c >= 2:
+            take_out(c - 2)
+        if c >= 3:
+            drain_out(c - 3)
+    for c in range(max(chunks - 3, 0), max(chunks - 2, 0)):
+        drain_out(c)
+    for c in range(max(chunks - 2, 0), chunks):
+        take_out(c)
+    for c in range(max(chunks - 2, 0), chunks):
+        drain_out(c)
 
 
 def on_device(tokens, w_query, key_value_weight, w_out, doc_lengths):
@@ -696,16 +765,15 @@
     return pl.pallas_call(
         functools.partial(layer_kernel, n, heads, out_cols, q_units),
         out_shape=jax.ShapeDtypeStruct((own, width), bf16),
-        in_specs=[
-            pl.BlockSpec(memory_space=pltpu.VMEM),
+        in_specs=[pl.BlockSpec(memory_space=pl.ANY)] * 4 + [
+            pl.BlockSpec(memory_space=pltpu.SMEM),
             pl.BlockSpec(memory_space=pl.ANY),
-            pl.BlockSpec(memory_space=pltpu.VMEM),
-            pl.BlockSpec(memory_space=pl.ANY),
-            pl.BlockSpec(memory_space=pltpu.SMEM),
-            pl.BlockSpec(memory_space=pltpu.VMEM),
         ],
-        out_specs=pl.BlockSpec(memory_space=pltpu.VMEM),
+        out_specs=pl.BlockSpec(memory_space=pl.ANY),
         scratch_shapes=[
+            pltpu.VMEM((own, width), bf16),
+            pltpu.VMEM(key_value_weight.shape, bf16),
+            pltpu.VMEM((1, HEAD_SIZE), f32),
             pltpu.VMEM((n * rows_in, kv_cols), bf16),
             pltpu.VMEM((q_units, n * rows_in, q_cols // q_units), bf16),
             pltpu.VMEM((2, 2, n, rows_out, col_width), bf16),
@@ -722,11 +790,13 @@
             pltpu.VMEM((2, block, HEAD_SIZE), f32),
             pltpu.VMEM((heads, own, col_width), bf16),
             pltpu.VMEM((own, width), bf16),
-            dma((units, 2, steps)),
+            dma((units, steps + 1)),
             dma((units, steps)),
             dma((units, 2, steps)),
             dma((1 + q_units,)),
             dma((1 + q_units,)),
+            dma((3,)),
+            dma((chunks, heads)),
             dma((3,)),
             dma((heads,)),
             dma((8,)),

time: 114 us -> 109 us (0.956)
  Pallas kernels: 110 us -> 105 us
    pallas_call x1, Pallas kernels: 110 us -> 105 us  [on_device(): pl.pallas_call(functools.partial(layer_kernel, n, heads, out_cols, q_unit...]
where the time goes in v3:
time: 109 us; the launch traced here: 107 us
  Pallas kernels  105 us (96%)
  local copies, waits for them, and re-layouts  2.29 us (2%)
    pallas_call x1, Pallas kernels, on_device(): pl.pallas_call(functools.partial(layer_kernel, n, heads, out_cols, q_unit...  105 us
    unnamed x1, local copies, waits for them, and re-layouts  2.29 us

profile of v3, /device:TPU:27, one launch (start us, length us, event | category | flops | bytes accessed | tf_op | source)
XLA Modules:
  0.0 107.2 jit_solution(12868166486601775783)
XLA Ops:
  0.0 104.9 %shard_map.64 = bf16[128,4096]{1,0:T(8,128)(2,1)} custom-call(bf16[128,4096]{1,0:T(8,128)(2,1)} %tok_ref.1, bf16[512,512]{1,0:T(8,128)(2,1)} %w_query_ref.1, bf16[512,2,128]{2,1,0:T(2,128)(2,1)} %w_keyval_ref.1, bf16[64,4096]{1,0:T(8,128)(2,1)} %w_out_ref.1, s32[16]{0:T(128)} %len_ref.1, f32[1,128]{1,0:T(1,128)} %constant.2.clone.freq_ref), custom_call_target="tpu_custom_call" | custom-call | tf_op jit(solution)/shard_map/pallas_call | solution.py:765
  104.9 2.3 %copy.8 = bf16[128,4096]{1,0:T(8,128)(2,1)} copy(bf16[128,4096]{1,0:T(8,128)(2,1)} %shard_map.64) | data formatting | bytes 2097152

commit v4 on v3

--- a/solution.py
+++ b/solution.py
@@ -25,7 +25,7 @@
     n, heads, out_cols, q_units,
     tok_ref, w_query_ref, w_keyval_ref, w_out_ref, len_ref, freq_ref, out_ref,
     tok_buf, kv_raw, freq_buf, w_kv, w_q, w_proj, kv_stage, act_stage, acts, qkv, query, kv, high, total, accum, mixed, rope, osend, obuf,
-    line_send, mate_send, recv, cross_send, local_sem, load_sem, store_sem, redis_send, redis_recv,
+    line_send, mate_send, recv, mate_recv, cross_send, local_sem, load_sem, store_sem, redis_send, redis_recv,
     act_send, act_recv, kv_send, kv_recv, kv_pass_send, mix_send, mix_recv, out_send, out_recv,
 ):
     f32, bf16 = jnp.float32, jnp.bfloat16
@@ -99,22 +99,31 @@
         at = row
         if direction == DOWN:
             at = jnp.where(row == z, steps, row)
-        return remote(ref, ref, line_send.at[u, at], recv.at[u, core, row], dev(x, y, z_, core))
+        return remote(ref, ref, line_send.at[u, at], recv.at[u, row], dev(x, y, z_, core))
 
     def mate_copy(u, row):
         ref = unit_ref(u, core, row)
-        return remote(ref, ref, mate_send.at[u, row], recv.at[u, core, row], mate)
-
-    def arrive(u, k, row):
-        ref = unit_ref(u, k, row)
-        remote(ref, ref, mate_send.at[u, 0], recv.at[u, k, row], mate).wait_recv()
+        return remote(ref, ref, mate_send.at[u], mate_recv.at[u], mate)
+
+    def mate_all(u):
+        if u == 0:
+            ref = w_kv.at[pl.ds(0, steps * rows_in)]
+        elif u < first_out:
+            ref = w_q.at[u - 1, pl.ds(0, steps * rows_in)]
+        else:
+            ref = w_proj.at[:, 0, :, :, pl.ds(out_first[u - first_out], out_cols[u - first_out])]
+        return remote(ref, ref, mate_send.at[u], mate_recv.at[u], mate)
+
+    def arrive(u, row):
+        ref = unit_ref(u, core, row)
+        remote(ref, ref, mate_send.at[u], recv.at[u, row], mate).wait_recv()
 
     def query_cols(u):
         return w_query_ref.at[:, pl.ds((u - 1) * unit_cols, unit_cols)]
 
     def cross_copy(u):
         src = kv_stage if u == 0 else query_cols(u)
-        return remote(src, unit_ref(u, x, z), cross_send.at[u], recv.at[u, x, z], dev(1 - x, y, z, 1 - core))
+        return remote(src, unit_ref(u, x, z), cross_send.at[u], recv.at[u, z], dev(1 - x, y, z, 1 - core))
 
     def keep_query(u):
         return pltpu.make_async_copy(query_cols(u), unit_ref(u, core, z), local_sem.at[u])
@@ -133,12 +142,16 @@
     def redis_peers():
         return [(1 - x, y), (x, 1 - y), (1 - x, 1 - y)]
 
-    def redis_copy(i, x_, y_):
+    def redis_copy(x_, y_):
         cols = pl.ds(pl.multiple_of((2 * y_ + x_) * col_width, col_width), col_width)
         return remote(
-            w_out_ref.at[:, cols], w_proj.at[y, core, b], redis_send.at[i], redis_recv.at[group],
+            w_out_ref.at[:, cols], w_proj.at[y, core, b], redis_send.at[0], redis_recv.at[0],
             dev(x_, y_, z, core),
         )
+
+    def redis_all():
+        ref = w_proj.at[0, 0, pl.ds(0, 3)]
+        return remote(ref, ref, redis_send.at[0], redis_recv.at[0], mate)
 
     def keep_out():
         cols = pl.ds(pl.multiple_of(group * col_width, col_width), col_width)
@@ -148,25 +161,23 @@
         if u == 0:
             @pl.when(apart == 1)
             def _():
-                arrive(u, core, z)
+                arrive(u, z)
         elif u < first_out:
             @pl.when(apart == 1)
             def _():
-                arrive(u, core, z)
+                arrive(u, z)
 
             @pl.when(apart == 0)
             def _():
                 keep_query(u).wait()
         elif u == first_out:
             keep_out().wait()
-            for x_, y_ in redis_peers():
-                ref = w_proj.at[y_, core, LINE * z + x_]
-                remote(ref, ref, redis_send.at[0], redis_recv.at[2 * y_ + x_], mate).wait_recv()
+            redis_all().wait_recv()
 
     def line_step(u, s):
         @pl.when(z - s >= 0)
         def _():
-            arrive(u, core, z - s)
+            arrive(u, z - s)
 
             @pl.when(z < steps - 1)
             def _():
@@ -176,7 +187,7 @@
 
         @pl.when(z + s <= steps - 1)
         def _():
-            arrive(u, core, z + s)
+            arrive(u, z + s)
 
             @pl.when(z > 0)
             def _():
@@ -204,11 +215,7 @@
             line_steps(u, low, high_)
 
     def mate_wait(u):
-        def one(row, _):
-            arrive(u, 1 - core, row)
-            return 0
-
-        lax.fori_loop(0, steps, one, 0)
+        mate_all(u).wait_recv()
 
     @pl.when(apart == 0)
     def _():
@@ -268,11 +275,11 @@
 
     act_copies = [
         act_own(0, 1, dev(x, 1 - y, z, x)),
-        act_own(1, 0, dev(1 - x, y, z, x)),
-        act_own(2, 0, dev(x, 1 - y, z, x)),
-        act_own(3, 1, dev(1 - x, y, z, x)),
+        act_own(0, 0, dev(1 - x, y, z, x)),
+        act_own(0, 0, dev(x, 1 - y, z, x)),
+        act_own(0, 1, dev(1 - x, y, z, x)),
     ]
-    act_mate = [act_own(4 + f, f, mate) for f in (0, 1)]
+    act_mate = [act_own(1, f, mate) for f in (0, 1)]
     act_copies[0].start()
     act_copies[2].start()
 
@@ -285,14 +292,14 @@
             copy.start()
         act_copies[3].start()
 
-    redis_copies = [redis_copy(i, x_, y_) for i, (x_, y_) in enumerate(redis_peers())]
+    redis_copies = [redis_copy(x_, y_) for x_, y_ in redis_peers()]
 
     relay_y = apart * y + (1 - apart) * (1 - y)
 
     def relay_copy(i, f):
         c = core if i == 0 else 1 - core
         to = dev(x, 1 - y, z, core) if f == 0 else dev(1 - x, y, z, core)
-        return act_copy(6 + i, 2 * relay_y + c, f, to)
+        return act_copy(2 + i, 2 * relay_y + c, f, to)
 
     def relay(i):
         for f in (0, 1):
@@ -527,9 +534,9 @@
     def mix_cols(u):
         return pl.ds((u - 1) * unit_cols, unit_cols)
 
-    def mix_copy(u, i, x_, y_):
+    def mix_copy(u, x_, y_):
         ref = mixed.at[group, :, mix_cols(u)]
-        return remote(ref, ref, mix_send.at[u - 1, i], mix_recv.at[u - 1, group], dev(x_, y_, z, core))
+        return remote(ref, ref, mix_send.at[u - 1], mix_recv.at[u - 1], dev(x_, y_, z, core))
 
     def attend(u):
         if reach <= 2:
@@ -537,8 +544,8 @@
         else:
             attend_own(u)
             finish_heads(u)
-        for i, (x_, y_) in enumerate(redis_peers()):
-            mix_copy(u, i, x_, y_).start()
+        for x_, y_ in redis_peers():
+            mix_copy(u, x_, y_).start()
 
     def finish_heads(u):
         def one(d, _):
@@ -552,11 +559,13 @@
             cols = slice(j * HEAD_SIZE, (j + 1) * HEAD_SIZE)
             mixed[group, :, cols] = (accum[:, cols] / total[j]).astype(bf16)
 
+    def mix_all(u):
+        ref = mixed.at[pl.ds(0, 3), :, mix_cols(u)]
+        return remote(ref, ref, mix_send.at[u - 1], mix_recv.at[u - 1], mate)
+
     def mix_wait():
         for u in range(1, first_out):
-            for x_, y_ in redis_peers():
-                ref = mixed.at[2 * y_ + x_, :, mix_cols(u)]
-                remote(ref, ref, mix_send.at[0, 0], mix_recv.at[u - 1, 2 * y_ + x_], mate).wait_recv()
+            mix_all(u).wait_recv()
 
     mate_wait(0)
     project(w_kv, slice(q_cols, q_cols + w_kv.shape[1]))
@@ -592,22 +601,17 @@
     @pl.when(inner)
     def _():
         line_step(first_out, 1)
+        own_start(first_out + 1)
+
+    attend(last_in)
+
+    @pl.when(inner)
+    def _():
+        line_steps(first_out, 2, steps)
         for u in range(first_out + 1, units):
-            own_start(u)
-
-    attend(last_in)
-
-    @pl.when(inner)
-    def _():
-        def one(s, _):
-            line_step(first_out, s)
-            for u in range(first_out + 1, units):
-                line_step(u, s - 1)
-            return 0
-
-        lax.fori_loop(2, steps, one, 0)
-        for u in range(first_out + 1, units):
-            line_step(u, steps - 1)
+            if u + 1 < units:
+                own_start(u + 1)
+            line_steps(u, 1, steps)
 
     def out_at(g, c):
         return pl.ds(pl.multiple_of(g * col_width + out_first[c], HEAD_SIZE), out_cols[c])
@@ -617,7 +621,7 @@
 
     def out_copy(c, r):
         return remote(
-            out_part(r, c), obuf.at[:, out_at(group, c)], out_send.at[c, r], out_recv.at[c, group],
+            out_part(r, c), obuf.at[:, out_at(group, c)], out_send.at[c], out_recv.at[c],
             dev(core, r // 2, z, r % 2),
         )
 
@@ -654,11 +658,14 @@
             @pl.when((row >= z) & (z > 0))
             def _():
                 line_copy(u, DOWN, row).wait_send()
-
-            mate_copy(u, row).wait_send()
             return 0
 
         lax.fori_loop(0, steps, one, 0)
+        mate_all(u).wait_send()
+
+    def act_all(i, count):
+        ref = acts.at[pl.ds(0, count)]
+        return remote(ref, ref, act_send.at[i], act_recv.at[0, 0], mate)
 
     def drain_in():
         for u in range(first_out):
@@ -668,11 +675,10 @@
         def _():
             for u in range(first_out):
                 cross_copy(u).wait_send()
-            for copy in act_mate:
-                copy.wait_send()
-
-        for copy in act_copies + redis_copies:
-            copy.wait_send()
+            act_all(1, 1).wait_send()
+
+        act_all(0, 2).wait_send()
+        redis_all().wait_send()
         for f in (0, 1):
             @pl.when(apart == 1 - f)
             def _():
@@ -694,32 +700,25 @@
 
         kv_each(1, reach // 2 + 1, kv_drain)
         for u in range(1, first_out):
-            for i, (x_, y_) in enumerate(redis_peers()):
-                mix_copy(u, i, x_, y_).wait_send()
-
-    def store_copy(c, g):
-        return pltpu.make_async_copy(
-            obuf.at[:, out_at(g, c)], out_ref.at[:, out_at(g, c)], store_sem.at[c, g]
-        )
+            mix_all(u).wait_send()
+
+    def out_each(c, body):
+        for count in (heads - 1, heads):
+            @pl.when(apart == count - heads + 1)
+            def _():
+                ref = obuf.at[:, pl.ds(0, count * out_cols[c])]
+                body(remote(ref, ref, out_send.at[c], out_recv.at[c], mate))
 
     def take_out(c):
+        out_each(c, lambda copy: copy.wait_recv())
         for g in range(heads):
-            @pl.when((apart == 1) | (group != g))
-            def _():
-                ref = obuf.at[:, out_at(g, c)]
-                remote(ref, ref, out_send.at[0, 0], out_recv.at[c, g], mate).wait_recv()
-
-            store_copy(c, g).start()
+            pltpu.make_async_copy(
+                obuf.at[:, out_at(g, c)], out_ref.at[:, out_at(g, c)], store_sem.at[c]
+            ).start()
 
     def drain_out(c):
         drain_unit(first_out + c)
-        for r in range(heads):
-            @pl.when(away(r))
-            def _():
-                out_copy(c, r).wait_send()
-
-        for g in range(heads):
-            store_copy(c, g).wait()
+        out_each(c, lambda copy: copy.wait_send())
 
     for c in range(chunks):
         outer_steps(first_out + c, 1, steps)
@@ -729,16 +728,12 @@
         project_out(c)
         if c == 0:
             drain_in()
-        if c >= 2:
-            take_out(c - 2)
-        if c >= 3:
-            drain_out(c - 3)
-    for c in range(max(chunks - 3, 0), max(chunks - 2, 0)):
+    for c in range(chunks):
         drain_out(c)
-    for c in range(max(chunks - 2, 0), chunks):
         take_out(c)
-    for c in range(max(chunks - 2, 0), chunks):
-        drain_out(c)
+    for c in range(chunks):
+        cols = pl.ds(0, heads * out_cols[c])
+        pltpu.make_async_copy(obuf.at[:, cols], out_ref.at[:, cols], store_sem.at[c]).wait()
 
 
 def on_device(tokens, w_query, key_value_weight, w_out, doc_lengths):
@@ -791,23 +786,24 @@
             pltpu.VMEM((heads, own, col_width), bf16),
             pltpu.VMEM((own, width), bf16),
             dma((units, steps + 1)),
+            dma((units,)),
             dma((units, steps)),
-            dma((units, 2, steps)),
+            dma((units,)),
             dma((1 + q_units,)),
             dma((1 + q_units,)),
             dma((3,)),
-            dma((chunks, heads)),
-            dma((3,)),
-            dma((heads,)),
-            dma((8,)),
+            dma((chunks,)),
+            dma((1,)),
+            dma((1,)),
+            dma((4,)),
             dma((2, heads)),
             dma((reach + 1,)),
             dma((reach + 1,)),
             dma((reach + 1,)),
-            dma((q_units, 3)),
-            dma((q_units, heads)),
-            dma((chunks, heads)),
-            dma((chunks, heads)),
+            dma((q_units,)),
+            dma((q_units,)),
+            dma((chunks,)),
+            dma((chunks,)),
         ],
         compiler_params=pltpu.CompilerParams(
             collective_id=0, has_side_effects=True, vmem_limit_bytes=60 * 1024 * 1024

time: 109 us -> 108 us (level)
  Pallas kernels: 105 us -> 103 us
    pallas_call x1, Pallas kernels: 105 us -> 103 us  [on_device(): pl.pallas_call(functools.partial(layer_kernel, n, heads, out_cols, q_unit...]
where the time goes in v4:
time: 108 us; the launch traced here: 106 us
  Pallas kernels  103 us (95%)
  local copies, waits for them, and re-layouts  2.29 us (2%)
    pallas_call x1, Pallas kernels, on_device(): pl.pallas_call(functools.partial(layer_kernel, n, heads, out_cols, q_unit...  103 us
    unnamed x1, local copies, waits for them, and re-layouts  2.29 us

profile of v4, /device:TPU:27, one launch (start us, length us, event | category | flops | bytes accessed | tf_op | source)
XLA Modules:
  0.0 105.6 jit_solution(10507947671159891972)
XLA Ops:
  0.0 103.3 %shard_map.64 = bf16[128,4096]{1,0:T(8,128)(2,1)} custom-call(bf16[128,4096]{1,0:T(8,128)(2,1)} %tok_ref.1, bf16[512,512]{1,0:T(8,128)(2,1)} %w_query_ref.1, bf16[512,2,128]{2,1,0:T(2,128)(2,1)} %w_keyval_ref.1, bf16[64,4096]{1,0:T(8,128)(2,1)} %w_out_ref.1, s32[16]{0:T(128)} %len_ref.1, f32[1,128]{1,0:T(1,128)} %constant.2.clone.freq_ref), custom_call_target="tpu_custom_call" | custom-call | tf_op jit(solution)/shard_map/pallas_call | solution.py:760
  103.3 2.3 %copy.8 = bf16[128,4096]{1,0:T(8,128)(2,1)} copy(bf16[128,4096]{1,0:T(8,128)(2,1)} %shard_map.64) | data formatting | bytes 2097152

commit v5 on v4

--- a/solution.py
+++ b/solution.py
@@ -24,7 +24,7 @@
 def layer_kernel(
     n, heads, out_cols, q_units,
     tok_ref, w_query_ref, w_keyval_ref, w_out_ref, len_ref, freq_ref, out_ref,
-    tok_buf, kv_raw, freq_buf, w_kv, w_q, w_proj, kv_stage, act_stage, acts, qkv, query, kv, high, total, accum, mixed, rope, osend, obuf,
+    tok_buf, kv_raw, freq_buf, w_kv, w_q, w_proj, kv_stage, act_stage, acts, qkv, query, kv, high, total, accum, mixed, rope, osend,
     line_send, mate_send, recv, mate_recv, cross_send, local_sem, load_sem, store_sem, redis_send, redis_recv,
     act_send, act_recv, kv_send, kv_recv, kv_pass_send, mix_send, mix_recv, out_send, out_recv,
 ):
@@ -234,6 +234,19 @@
     def _():
         kv_stage[...] = own_kv
 
+    pl.semaphore_wait(barrier, 7 + 2 * near)
+
+    @pl.when(apart == 0)
+    def _():
+        own_start(0)
+        own_wait(1)
+        own_start(1)
+
+    @pl.when(apart == 1)
+    def _():
+        for u in range(2):
+            cross_copy(u).start()
+
     loads[1].wait()
     values = tok_buf[...].astype(f32)
     normed = (
@@ -244,19 +257,6 @@
     @pl.when(apart == 0)
     def _():
         acts[h] = normed
-
-    pl.semaphore_wait(barrier, 7 + 2 * near)
-
-    @pl.when(apart == 0)
-    def _():
-        own_start(0)
-        own_wait(1)
-        own_start(1)
-
-    @pl.when(apart == 1)
-    def _():
-        for u in range(2):
-            cross_copy(u).start()
 
     act_cols = [(0, left), (left, width - left)]
 
@@ -619,35 +619,47 @@
     def out_part(r, c):
         return osend.at[r, :, pl.ds(out_first[c], out_cols[c])]
 
-    def out_copy(c, r):
+    def out_copy(c, y_, c_):
         return remote(
-            out_part(r, c), obuf.at[:, out_at(group, c)], out_send.at[c], out_recv.at[c],
-            dev(core, r // 2, z, r % 2),
+            out_part(2 * y_ + c_, c), out_ref.at[:, out_at(group, c)], out_send.at[c], out_recv.at[c],
+            dev(core, y_, z, c_),
         )
 
-    def away(r):
-        return (apart == 1) | (h != r)
+    def keep_result(c):
+        return pltpu.make_async_copy(out_part(h, c), out_ref.at[:, out_at(group, c)], store_sem.at[c])
 
     def project_out(c):
         cols = slice(out_first[c], out_first[c] + out_cols[c])
-        result = None
+        rights = []
         for g in range(heads):
             right = w_proj[g // 2, g % 2, :, :, cols]
             if right.shape[1] % 16:
                 right = right.astype(f32).reshape(-1, out_cols[c]).astype(bf16)
             else:
                 right = right.reshape(-1, out_cols[c])
-            term = jnp.dot(mixed[g], right, preferred_element_type=f32)
-            result = term if result is None else result + term
-        osend[:, :, cols] = result.astype(bf16).reshape(heads, own, out_cols[c])
-        for r in range(heads):
-            @pl.when(away(r))
-            def _():
-                out_copy(c, r).start()
-
-        @pl.when(apart == 0)
-        def _():
-            obuf[:, out_at(group, c)] = osend[h, :, cols]
+            rights.append(right)
+        for far in (1, 0):
+            y_ = far * (1 - y) + (1 - far) * y
+            rows = pl.ds(pl.multiple_of(y_ * 2 * own, 2 * own), 2 * own)
+            result = None
+            for g in range(heads):
+                term = jnp.dot(mixed[g, rows, :], rights[g], preferred_element_type=f32)
+                result = term if result is None else result + term
+            osend[pl.ds(2 * y_, 2), :, cols] = result.astype(bf16).reshape(2, own, out_cols[c])
+            if far:
+                for c_ in (0, 1):
+                    out_copy(c, y_, c_).start()
+                continue
+
+            @pl.when(apart == 1)
+            def _():
+                for c_ in (0, 1):
+                    out_copy(c, y, c_).start()
+
+            @pl.when(apart == 0)
+            def _():
+                out_copy(c, y, 1 - core).start()
+                keep_result(c).start()
 
     def drain_unit(u):
         def one(row, _):
@@ -706,19 +718,8 @@
         for count in (heads - 1, heads):
             @pl.when(apart == count - heads + 1)
             def _():
-                ref = obuf.at[:, pl.ds(0, count * out_cols[c])]
+                ref = out_ref.at[:, pl.ds(0, count * out_cols[c])]
                 body(remote(ref, ref, out_send.at[c], out_recv.at[c], mate))
-
-    def take_out(c):
-        out_each(c, lambda copy: copy.wait_recv())
-        for g in range(heads):
-            pltpu.make_async_copy(
-                obuf.at[:, out_at(g, c)], out_ref.at[:, out_at(g, c)], store_sem.at[c]
-            ).start()
-
-    def drain_out(c):
-        drain_unit(first_out + c)
-        out_each(c, lambda copy: copy.wait_send())
 
     for c in range(chunks):
         outer_steps(first_out + c, 1, steps)
@@ -729,11 +730,14 @@
         if c == 0:
             drain_in()
     for c in range(chunks):
-        drain_out(c)
-        take_out(c)
+        drain_unit(first_out + c)
+        out_each(c, lambda copy: copy.wait_send())
     for c in range(chunks):
-        cols = pl.ds(0, heads * out_cols[c])
-        pltpu.make_async_copy(obuf.at[:, cols], out_ref.at[:, cols], store_sem.at[c]).wait()
+        out_each(c, lambda copy: copy.wait_recv())
+
+        @pl.when(apart == 0)
+        def _():
+            keep_result(c).wait()
 
 
 def on_device(tokens, w_query, key_value_weight, w_out, doc_lengths):
@@ -784,7 +788,6 @@
             pltpu.VMEM((heads, block, q_cols), bf16),
             pltpu.VMEM((2, block, HEAD_SIZE), f32),
             pltpu.VMEM((heads, own, col_width), bf16),
-            pltpu.VMEM((own, width), bf16),
             dma((units, steps + 1)),
             dma((units,)),
             dma((units, steps)),

time: 108 us -> 106 us (0.981); the launches traced: 106 us -> 105 us
  no operation moved by 1% of the time
where the time goes in v5:
time: 106 us; the launch traced here: 105 us
  Pallas kernels  102 us (96%)
  local copies, waits for them, and re-layouts  2.29 us (2%)
    pallas_call x1, Pallas kernels, on_device(): pl.pallas_call(functools.partial(layer_kernel, n, heads, out_cols, q_unit...  102 us
    unnamed x1, local copies, waits for them, and re-layouts  2.29 us

profile of v5, /device:TPU:27, one launch (start us, length us, event | category | flops | bytes accessed | tf_op | source)
XLA Modules:
  0.0 104.8 jit_solution(7060052694755187193)
XLA Ops:
  0.0 102.5 %shard_map.64 = bf16[128,4096]{1,0:T(8,128)(2,1)} custom-call(bf16[128,4096]{1,0:T(8,128)(2,1)} %tok_ref.1, bf16[512,512]{1,0:T(8,128)(2,1)} %w_query_ref.1, bf16[512,2,128]{2,1,0:T(2,128)(2,1)} %w_keyval_ref.1, bf16[64,4096]{1,0:T(8,128)(2,1)} %w_out_ref.1, s32[16]{0:T(128)} %len_ref.1, f32[1,128]{1,0:T(1,128)} %constant.2.clone.freq_ref), custom_call_target="tpu_custom_call" | custom-call | tf_op jit(solution)/shard_map/pallas_call | solution.py:764
  102.5 2.3 %copy.8 = bf16[128,4096]{1,0:T(8,128)(2,1)} copy(bf16[128,4096]{1,0:T(8,128)(2,1)} %shard_map.64) | data formatting | bytes 2097152

commit v6 on v5

--- a/solution.py
+++ b/solution.py
@@ -24,7 +24,7 @@
 def layer_kernel(
     n, heads, out_cols, q_units,
     tok_ref, w_query_ref, w_keyval_ref, w_out_ref, len_ref, freq_ref, out_ref,
-    tok_buf, kv_raw, freq_buf, w_kv, w_q, w_proj, kv_stage, act_stage, acts, qkv, query, kv, high, total, accum, mixed, rope, osend,
+    tok_buf, kv_raw, freq_buf, len_buf, w_kv, w_q, w_proj, kv_stage, act_stage, acts, qkv, query, kv, high, total, accum, mixed, rope, osend,
     line_send, mate_send, recv, mate_recv, cross_send, local_sem, load_sem, store_sem, redis_send, redis_recv,
     act_send, act_recv, kv_send, kv_recv, kv_pass_send, mix_send, mix_recv, out_send, out_recv,
 ):
@@ -80,7 +80,7 @@
     near = jnp.minimum(z, span) + jnp.minimum(steps - 1 - z, span)
     loads = [
         pltpu.make_async_copy(src, dst, load_sem.at[i])
-        for i, (src, dst) in enumerate([(w_keyval_ref, kv_raw), (tok_ref, tok_buf), (freq_ref, freq_buf)])
+        for i, (src, dst) in enumerate([(w_keyval_ref, kv_raw), (tok_ref, tok_buf), (freq_ref, freq_buf), (len_ref, len_buf)])
     ]
     for load in loads:
         load.start()
@@ -323,14 +323,15 @@
         own_wait(0)
         own_start(0)
 
+    loads[2].wait()
+    loads[3].wait()
     pos = block_id * block + lax.broadcasted_iota(jnp.int32, (block, 1), 0)
     start = jnp.zeros((block, 1), jnp.int32)
     end = jnp.int32(0)
     for i in range(len_ref.shape[0]):
-        size = len_ref[i]
+        size = len_buf[i]
         end = end + size
         start = start + jnp.where(pos >= end, size, 0)
-    loads[2].wait()
     angle = (pos - start).astype(f32) * freq_buf[...]
     lane = lax.broadcasted_iota(jnp.int32, (block, HEAD_SIZE), 1)
     rope[0] = jnp.cos(angle)
@@ -764,15 +765,13 @@
     return pl.pallas_call(
         functools.partial(layer_kernel, n, heads, out_cols, q_units),
         out_shape=jax.ShapeDtypeStruct((own, width), bf16),
-        in_specs=[pl.BlockSpec(memory_space=pl.ANY)] * 4 + [
-            pl.BlockSpec(memory_space=pltpu.SMEM),
-            pl.BlockSpec(memory_space=pl.ANY),
-        ],
+        in_specs=[pl.BlockSpec(memory_space=pl.ANY)] * 6,
         out_specs=pl.BlockSpec(memory_space=pl.ANY),
         scratch_shapes=[
             pltpu.VMEM((own, width), bf16),
             pltpu.VMEM(key_value_weight.shape, bf16),
             pltpu.VMEM((1, HEAD_SIZE), f32),
+            pltpu.SMEM(doc_lengths.shape, jnp.int32),
             pltpu.VMEM((n * rows_in, kv_cols), bf16),
             pltpu.VMEM((q_units, n * rows_in, q_cols // q_units), bf16),
             pltpu.VMEM((2, 2, n, rows_out, col_width), bf16),
@@ -794,7 +793,7 @@
             dma((units,)),
             dma((1 + q_units,)),
             dma((1 + q_units,)),
-            dma((3,)),
+            dma((4,)),
             dma((chunks,)),
             dma((1,)),
             dma((1,)),

time: 106 us -> 105 us (level)
  no operation moved by 1% of the time
where the time goes in v6:
time: 105 us; the launch traced here: 104 us
  Pallas kernels  102 us (97%)
  local copies, waits for them, and re-layouts  2.29 us (2%)
    pallas_call x1, Pallas kernels, on_device(): pl.pallas_call(functools.partial(layer_kernel, n, heads, out_cols, q_unit...  102 us
    unnamed x1, local copies, waits for them, and re-layouts  2.29 us

profile of v6, /device:TPU:27, one launch (start us, length us, event | category | flops | bytes accessed | tf_op | source)
XLA Modules:
  0.0 104.0 jit_solution(9696144893582987829)
XLA Ops:
  0.0 101.7 %shard_map.64 = bf16[128,4096]{1,0:T(8,128)(2,1)} custom-call(bf16[128,4096]{1,0:T(8,128)(2,1)} %tok_ref.1, bf16[512,512]{1,0:T(8,128)(2,1)} %w_query_ref.1, bf16[512,2,128]{2,1,0:T(2,128)(2,1)} %w_keyval_ref.1, bf16[64,4096]{1,0:T(8,128)(2,1)} %w_out_ref.1, s32[16]{0:T(128)} %len_ref.1, f32[1,128]{1,0:T(1,128)} %constant.2.clone.freq_ref), custom_call_target="tpu_custom_call" | custom-call | tf_op jit(solution)/shard_map/pallas_call | solution.py:765
  101.7 2.3 %copy.8 = bf16[128,4096]{1,0:T(8,128)(2,1)} copy(bf16[128,4096]{1,0:T(8,128)(2,1)} %shard_map.64) | data formatting | bytes 2097152

commit v7 on v6

--- a/solution.py
+++ b/solution.py
@@ -67,16 +67,15 @@
         pl.semaphore_signal(
             barrier, inc=1, device_id=dev((x + dx) % 2, (y + dy) % 2, z, (core + dc) % 2), device_id_type=MESH
         )
-    span = (reach + 1) // 2
+    span = max(reach // 2, 1)
     for d in range(1, span + 1):
-        for c_ in (0, 1):
-            @pl.when(z + d < steps)
-            def _():
-                pl.semaphore_signal(barrier, inc=1, device_id=dev(x, y, z + d, c_), device_id_type=MESH)
-
-            @pl.when(z - d >= 0)
-            def _():
-                pl.semaphore_signal(barrier, inc=1, device_id=dev(x, y, z - d, c_), device_id_type=MESH)
+        @pl.when(z + d < steps)
+        def _():
+            pl.semaphore_signal(barrier, inc=1, device_id=dev(x, y, z + d, core), device_id_type=MESH)
+
+        @pl.when(z - d >= 0)
+        def _():
+            pl.semaphore_signal(barrier, inc=1, device_id=dev(x, y, z - d, core), device_id_type=MESH)
     near = jnp.minimum(z, span) + jnp.minimum(steps - 1 - z, span)
     loads = [
         pltpu.make_async_copy(src, dst, load_sem.at[i])
@@ -234,7 +233,7 @@
     def _():
         kv_stage[...] = own_kv
 
-    pl.semaphore_wait(barrier, 7 + 2 * near)
+    pl.semaphore_wait(barrier, 7 + near)
 
     @pl.when(apart == 0)
     def _():

time: 105 us -> 105 us (level)
  no operation moved by 1% of the time
where the time goes in v7:
time: 105 us; the launch traced here: 104 us
  Pallas kernels  102 us (97%)
  local copies, waits for them, and re-layouts  2.29 us (2%)
    pallas_call x1, Pallas kernels, on_device(): pl.pallas_call(functools.partial(layer_kernel, n, heads, out_cols, q_unit...  102 us
    unnamed x1, local copies, waits for them, and re-layouts  2.29 us

profile of v7, /device:TPU:27, one launch (start us, length us, event | category | flops | bytes accessed | tf_op | source)
XLA Modules:
  0.0 104.0 jit_solution(16357996222268586302)
XLA Ops:
  0.0 101.7 %shard_map.64 = bf16[128,4096]{1,0:T(8,128)(2,1)} custom-call(bf16[128,4096]{1,0:T(8,128)(2,1)} %tok_ref.1, bf16[512,512]{1,0:T(8,128)(2,1)} %w_query_ref.1, bf16[512,2,128]{2,1,0:T(2,128)(2,1)} %w_keyval_ref.1, bf16[64,4096]{1,0:T(8,128)(2,1)} %w_out_ref.1, s32[16]{0:T(128)} %len_ref.1, f32[1,128]{1,0:T(1,128)} %constant.2.clone.freq_ref), custom_call_target="tpu_custom_call" | custom-call | tf_op jit(solution)/shard_map/pallas_call | solution.py:764
  101.7 2.3 %copy.8 = bf16[128,4096]{1,0:T(8,128)(2,1)} copy(bf16[128,4096]{1,0:T(8,128)(2,1)} %shard_map.64) | data formatting | bytes 2097152
